TPU v7x, 512 devices: a whole 4x8x8 slice. The times are simulated.
512 devices in a mesh: px: 16 (over y_lo, x, core), py: 32 (over y_hi, z).
Axes of the slice: x: 4, y: 8 (y_hi: 4, y_lo: 2; y = y_hi * 2 + y_lo), z: 8, core: 2. Of those that a mesh axis runs over, the one named last changes fastest.
Arguments:
- metric: bfloat16 [3, 640, 24, 4096], P(None, 'px', None, 'py'), may hold values from 0.25 to 24
- helmholtz: bfloat16 [640, 24, 4096], P('px', None, 'py'), may hold values from 1 to 30
- forcing: bfloat16 [640, 24, 4096], P('px', None, 'py'), may hold values from -6 to 6
- orientation: int32 [640, 4096], P('px', 'py'), may hold values 0 or 1
- start_x: float32 [640, 24, 4096], P('px', None, 'py'), may hold values from -6 to 6
- start_y: float32 [640, 24, 4096], P('px', None, 'py'), may hold values from -6 to 6
- start_z: float32 [640, 25, 4096], P('px', None, 'py'), may hold values from -6 to 6
Outputs:
- trace_x: float32 [640, 24, 4096], P('px', None, 'py')
- trace_y: float32 [640, 24, 4096], P('px', None, 'py')
- trace_z: float32 [640, 25, 4096], P('px', None, 'py')
- pressure: float32 [640, 24, 4096], P('px', None, 'py')
All inputs are finite; a program needn't handle non-finite values. No bound on the sum of `orientation` on one device may be relied on, other than what follows from the above.
Results may differ from a plain program's by a relative error of at most 0.0003.
Values sent between devices are 32-bit elements; how exact they have to be, the bound alone decides.
A program may use at most 64 MiB of HBM per device.

v0:
```python
import functools

import jax
import jax.numpy as jnp
from jax import lax
from jax.sharding import Mesh
from jax.sharding import PartitionSpec as P

ITERS = 2
PX = ("px_0", "px_1", "px_2")
PY = ("py_0", "py_1")
PX_PY = ("px_0", "px_1", "px_2", "py_0", "py_1")


def shifted(x, axis, by):
    devices = lax.axis_size(axis)
    return lax.ppermute(x, axis, [(i, (i + by) % devices) for i in range(devices)])


def extended(cells, sides, width):
    for axis, dim in sides:
        count = lax.axis_size(axis)
        head = lax.slice_in_dim(cells, 0, width, axis=dim)
        tail = lax.slice_in_dim(cells, cells.shape[dim] - width, cells.shape[dim], axis=dim)
        cells = jnp.concatenate(
            [
                lax.ppermute(tail, axis, [(i, (i + 1) % count) for i in range(count)]),
                cells,
                lax.ppermute(head, axis, [((i + 1) % count, i) for i in range(count)]),
            ],
            axis=dim,
        )
    return cells


def one_axis_at_a_time(x, axes):
    return functools.reduce(lax.psum, axes, x)


def coefficients(metric, helmholtz, orientation):
    metric_x = metric[0].astype(jnp.float32)
    metric_y = metric[1].astype(jnp.float32)
    metric_z = metric[2].astype(jnp.float32)
    turned = (orientation == 1)[:, None, :]
    inverse_x = 1.0 / jnp.where(turned, metric_y, metric_x)
    inverse_y = 1.0 / jnp.where(turned, metric_x, metric_y)
    inverse_z = 1.0 / metric_z
    denominator = helmholtz.astype(jnp.float32) + 2.0 * (
        3.0 * inverse_x + 3.0 * inverse_y + 3.0 * inverse_z
    )
    return (inverse_x, inverse_y, inverse_z, denominator)


def element(
    trace_west, trace_east, trace_south, trace_north, trace_bottom, trace_top, coeffs, source
):
    inverse_x, inverse_y, inverse_z, denominator = coeffs
    weight_x = 3.0 * inverse_x
    weight_y = 3.0 * inverse_y
    weight_z = 3.0 * inverse_z
    gathered = (
        weight_x * (trace_west + trace_east)
        + weight_y * (trace_south + trace_north)
        + weight_z * (trace_bottom + trace_top)
    )
    pressure = (source + gathered) / denominator
    flux_west = inverse_x * (2.0 * trace_west + trace_east) - weight_x * pressure
    flux_east = inverse_x * (trace_west + 2.0 * trace_east) - weight_x * pressure
    flux_south = inverse_y * (2.0 * trace_south + trace_north) - weight_y * pressure
    flux_north = inverse_y * (trace_south + 2.0 * trace_north) - weight_y * pressure
    flux_bottom = inverse_z * (2.0 * trace_bottom + trace_top) - weight_z * pressure
    flux_top = inverse_z * (trace_bottom + 2.0 * trace_top) - weight_z * pressure
    return (flux_west, flux_east, flux_south, flux_north, flux_bottom, flux_top, pressure)


def stack_vertical(flux_bottom, flux_top):
    zero_layer = jnp.zeros_like(flux_bottom[:, :1])
    return jnp.concatenate([flux_bottom, zero_layer], 1) + jnp.concatenate(
        [zero_layer, flux_top], 1
    )


def seeded(field_x, field_y):
    from_east = shifted(field_x[:1], PX, -1)
    from_north = shifted(field_y[:, :, :1], PY, -1)
    return (jnp.concatenate([field_x, from_east], 0), jnp.concatenate([field_y, from_north], 2))


def shared_apply(fields, coeffs, source):
    wide_x, wide_y, field_z = fields
    fluxes = element(
        wide_x[:-1],
        wide_x[1:],
        wide_y[:, :, :-1],
        wide_y[:, :, 1:],
        field_z[:, :-1],
        field_z[:, 1:],
        coeffs,
        source,
    )
    zero_x = jnp.zeros_like(fluxes[0][:1])
    part_x = jnp.concatenate([fluxes[0], zero_x], 0) + jnp.concatenate([zero_x, fluxes[1]], 0)
    zero_y = jnp.zeros_like(fluxes[2][:, :, :1])
    part_y = jnp.concatenate([fluxes[2], zero_y], 2) + jnp.concatenate([zero_y, fluxes[3]], 2)
    seam_pair = jnp.concatenate([part_x[:1], part_x[-1:]], 0)
    around_x = extended(seam_pair, ((PX, 0),), 1)
    sum_x = jnp.concatenate(
        [part_x[:1] + around_x[0:1], part_x[1:-1], part_x[-1:] + around_x[3:4]], 0
    )
    edge_pair = jnp.concatenate([part_y[:, :, :1], part_y[:, :, -1:]], 2)
    around_y = extended(edge_pair, ((PY, 2),), 1)
    sum_y = jnp.concatenate(
        [
            part_y[:, :, :1] + around_y[:, :, 0:1],
            part_y[:, :, 1:-1],
            part_y[:, :, -1:] + around_y[:, :, 3:4],
        ],
        2,
    )
    return (sum_x, sum_y, stack_vertical(fluxes[4], fluxes[5]))


def shared_pressure(fields, coeffs, source):
    wide_x, wide_y, field_z = fields
    return element(
        wide_x[:-1],
        wide_x[1:],
        wide_y[:, :, :-1],
        wide_y[:, :, 1:],
        field_z[:, :-1],
        field_z[:, 1:],
        coeffs,
        source,
    )[6]


def shared_inner(first_vec, second_vec):
    part_x = jnp.sum(first_vec[0][:-1] * second_vec[0][:-1])
    part_y = jnp.sum(first_vec[1][:, :, :-1] * second_vec[1][:, :, :-1])
    return part_x + part_y + jnp.sum(first_vec[2] * second_vec[2])


def combine(first_vec, scale, second_vec):
    return tuple((member + scale * other for member, other in zip(first_vec, second_vec)))


def pair_sums(norm_part, curve_part):
    return (one_axis_at_a_time(norm_part, PX_PY), one_axis_at_a_time(curve_part, PX_PY))


def local(metric, helmholtz, forcing, orientation, start_x, start_y, start_z):
    coeffs = coefficients(metric, helmholtz, orientation)
    source = forcing.astype(jnp.float32)
    wide_x, wide_y = seeded(start_x, start_y)
    traces = (wide_x, wide_y, start_z)
    sums = shared_apply(traces, coeffs, source)
    residual = tuple((-member for member in sums))
    applied = shared_apply(residual, coeffs, 0.0)
    norm_now, curvature_sum = pair_sums(
        shared_inner(residual, residual), shared_inner(residual, applied)
    )
    step_size = norm_now / curvature_sum
    direction = residual
    image_dir = applied
    for iteration in range(ITERS):
        traces = combine(traces, step_size, direction)
        residual = combine(residual, -step_size, image_dir)
        if iteration + 1 < ITERS:
            applied = shared_apply(residual, coeffs, 0.0)
            norm_next, curvature_sum = pair_sums(
                shared_inner(residual, residual), shared_inner(residual, applied)
            )
            beta_ratio = norm_next / norm_now
            step_size = norm_next / (curvature_sum - beta_ratio * norm_next / step_size)
            direction = combine(residual, beta_ratio, direction)
            image_dir = combine(applied, beta_ratio, image_dir)
            norm_now = norm_next
    pressure = shared_pressure(traces, coeffs, source)
    return (traces[0][:-1], traces[1][:, :, :-1], traces[2], pressure)


def solution(mesh):
    finer = Mesh(mesh.devices.reshape(2, 4, 2, 4, 8), ("px_0", "px_1", "px_2", "py_0", "py_1"))
    placed = (
        P(None, PX, None, PY),
        P(PX, None, PY),
        P(PX, None, PY),
        P(PX, PY),
        P(PX, None, PY),
        P(PX, None, PY),
        P(PX, None, PY),
    )
    return jax.shard_map(
        local,
        mesh=finer,
        in_specs=placed,
        out_specs=(P(PX, None, PY), P(PX, None, PY), P(PX, None, PY), P(PX, None, PY)),
        check_vma=False,
    )
```

profile of v0, /device:TPU:1, one launch (start us, length us, event | category | flops | bytes accessed | tf_op | source)
XLA Modules:
  0.0 301.8 jit_solution(16089378112215844726)
XLA Ops:
  0.6 0.7 slice.163
  1.3 8.7 %collective-permute-start = (f32[1,24,128]{2,1,0:T(8,128)S(1)}, f32[1,24,128]{2,1,0:T(8,128)S(1)}, u32[]{:S(2)}, u32[]{:S(2)}) collective-permute-start(f32[1,24,128]{2,1,0:T(8,128)S(1)} %slice.163), channel_id=1, source_target_pairs={{0,480},{32,0},{64,32},{96,64},{128,96},{160,128},{192,160},{224,1... | collective-permute-start | bytes 36872 | tf_op jit(solution)/shard_map/ppermute | solution.py:17
  10.1 9.1 %collective-permute-start.1 = (f32[40,24,1]{2,1,0:T(8,128)}, f32[40,24,1]{2,1,0:T(8,128)S(1)}, u32[]{:S(2)}, u32[]{:S(2)}) collective-permute-start(f32[40,24,1]{2,1,0:T(8,128)} %bitcast.144), channel_id=1, source_target_pairs={{0,31},{1,0},{2,1},{3,2},{4,3},{5,4},{6,5},{7,6},{8,7},{9,8},{10,9... | collective-permute-start | bytes 11528 | tf_op jit(solution)/shard_map/ppermute | solution.py:17
  19.3 1.1 constant_dynamic-update-slice_fusion.1
  20.4 1.0 copy-done.23
  21.5 17.4 %collective-permute-done.1 = f32[40,24,1]{2,1,0:T(8,128)S(1)} collective-permute-done((f32[40,24,1]{2,1,0:T(8,128)}, f32[40,24,1]{2,1,0:T(8,128)S(1)}, u32[]{:S(2)}, u32[]{:S(2)}) %collective-permute-start.1) | collective-permute-done | bytes 3872 | tf_op jit(solution)/shard_map/ppermute | solution.py:17
  40.7 5.6 %collective-permute-start.2 = (f32[1,24,128]{2,1,0:T(8,128)S(1)}, f32[1,24,128]{2,1,0:T(8,128)S(1)}, u32[]{:S(2)}, u32[]{:S(2)}) collective-permute-start(f32[1,24,128]{2,1,0:T(8,128)S(1)} %pad_add_fusion.11), channel_id=1, source_target_pairs={{0,32},{32,64},{64,96},{96,128},{128,160},{160,192},{192,224},{224... | collective-permute-start | bytes 36872 | tf_op jit(solution)/shard_map/ppermute | solution.py:27
  46.5 1.9 collective-permute-start.4
  48.4 0.9 multiply_reduce_fusion.3
  49.4 19.8 %collective-permute-done.4 = f32[40,24,1]{2,1,0:T(8,128)S(1)} collective-permute-done((f32[40,24,1]{2,1,0:T(8,128)S(1)}, f32[40,24,1]{2,1,0:T(8,128)S(1)}, u32[]{:S(2)}, u32[]{:S(2)}) %collective-permute-start.4) | collective-permute-done | bytes 3872 | tf_op jit(solution)/shard_map/ppermute | solution.py:27
  69.5 1.9 collective-permute-start.5
  71.5 12.2 %collective-permute-done.5 = f32[40,24,1]{2,1,0:T(8,128)S(1)} collective-permute-done((f32[40,24,1]{2,1,0:T(8,128)S(1)}, f32[40,24,1]{2,1,0:T(8,128)S(1)}, u32[]{:S(2)}, u32[]{:S(2)}) %collective-permute-start.5) | collective-permute-done | bytes 3872 | tf_op jit(solution)/shard_map/ppermute | solution.py:29
  83.8 3.2 %collective-permute-start.3 = (f32[1,24,128]{2,1,0:T(8,128)S(1)}, f32[1,24,128]{2,1,0:T(8,128)S(1)}, u32[]{:S(2)}, u32[]{:S(2)}) collective-permute-start(f32[1,24,128]{2,1,0:T(8,128)S(1)} %get-tuple-element.54), channel_id=1, source_target_pairs={{32,0},{64,32},{96,64},{128,96},{160,128},{192,160},{224,192},{256... | collective-permute-start | bytes 36872 | tf_op jit(solution)/shard_map/ppermute | solution.py:29
  87.4 2.1 collective-permute-done.3
  91.5 1.9 collective-permute-start.6
  93.6 6.2 %collective-permute-start.9 = (f32[40,24,1]{2,1,0:T(8,128)S(1)}, f32[40,24,1]{2,1,0:T(8,128)S(1)}, u32[]{:S(2)}, u32[]{:S(2)}) collective-permute-start(f32[40,24,1]{2,1,0:T(8,128)S(1)} %fusion.9), channel_id=1, source_target_pairs={{1,0},{2,1},{3,2},{4,3},{5,4},{6,5},{7,6},{8,7},{9,8},{10,9},{11,1... | collective-permute-start | bytes 11528 | tf_op jit(solution)/shard_map/ppermute | solution.py:29
  99.9 0.8 multiply_reduce_fusion.2
  100.9 4.8 %collective-permute-done.9 = f32[40,24,1]{2,1,0:T(8,128)S(1)} collective-permute-done((f32[40,24,1]{2,1,0:T(8,128)S(1)}, f32[40,24,1]{2,1,0:T(8,128)S(1)}, u32[]{:S(2)}, u32[]{:S(2)}) %collective-permute-start.9) | collective-permute-done | bytes 3872 | tf_op jit(solution)/shard_map/ppermute | solution.py:29
  105.6 1.0 fusion.32
  106.6 1.9 collective-permute-start.7
  108.6 13.7 %collective-permute-done.7 = f32[40,24,1]{2,1,0:T(8,128)S(1)} collective-permute-done((f32[40,24,1]{2,1,0:T(8,128)S(1)}, f32[40,24,1]{2,1,0:T(8,128)S(1)}, u32[]{:S(2)}, u32[]{:S(2)}) %collective-permute-start.7) | collective-permute-done | bytes 3872 | tf_op jit(solution)/shard_map/ppermute | solution.py:27
  122.4 0.9 fusion.19
  123.9 0.8 fusion.18
  128.5 19.7 %collective-permute-start.8 = (f32[1,24,128]{2,1,0:T(8,128)}, f32[1,24,128]{2,1,0:T(8,128)}, u32[]{:S(2)}, u32[]{:S(2)}) collective-permute-start(f32[1,24,128]{2,1,0:T(8,128)} %get-tuple-element.48), channel_id=1, source_target_pairs={{32,0},{64,32},{96,64},{128,96},{160,128},{192,160},{224,192},{256... | collective-permute-start | bytes 36872 | tf_op jit(solution)/shard_map/ppermute | solution.py:29
  148.3 11.6 %all-reduce.27 = (f32[]{:T(128)}, f32[]{:T(128)}) all-reduce(f32[]{:T(128)S(6)} %add.345, f32[]{:T(128)S(6)} %add.363), channel_id=1, replica_groups=mesh['px_0'=2,'px_1'=4,'px_2'=2,'py_0'=4,'py_1'=8] {'px_0'}, use_global_device_ids=true, to_apply=%region_3.4 | all-reduce | flops 2 | bytes 16 | tf_op jit(solution)/shard_map/psum | solution.py:37
  159.9 17.0 %all-reduce.23 = (f32[]{:T(128)}, f32[]{:T(128)}) all-reduce(f32[]{:T(128)} %get-tuple-element.36, f32[]{:T(128)} %get-tuple-element.37), channel_id=1, replica_groups=mesh['px_0'=2,'px_1'=4,'px_2'=2,'py_0'=4,'py_1'=8] {'px_1'}, use_global_device_ids=true, to_apply=%region_4.5 | all-reduce | flops 2 | bytes 16 | tf_op jit(solution)/shard_map/psum | solution.py:37
  176.9 7.6 %all-reduce.25 = (f32[]{:T(128)}, f32[]{:T(128)}) all-reduce(f32[]{:T(128)} %get-tuple-element.28, f32[]{:T(128)} %get-tuple-element.29), channel_id=1, replica_groups=mesh['px_0'=2,'px_1'=4,'px_2'=2,'py_0'=4,'py_1'=8] {'px_2'}, use_global_device_ids=true, to_apply=%region_5.6 | all-reduce | flops 2 | bytes 16 | tf_op jit(solution)/shard_map/psum | solution.py:37
  184.5 7.7 %all-reduce.21 = (f32[]{:T(128)}, f32[]{:T(128)}) all-reduce(f32[]{:T(128)} %get-tuple-element.32, f32[]{:T(128)} %get-tuple-element.33), channel_id=1, replica_groups=mesh['px_0'=2,'px_1'=4,'px_2'=2,'py_0'=4,'py_1'=8] {'py_0'}, use_global_device_ids=true, to_apply=%region_6.7 | all-reduce | flops 2 | bytes 16 | tf_op jit(solution)/shard_map/psum | solution.py:37
  192.2 11.4 %all-reduce.19 = (f32[]{:T(128)}, f32[]{:T(128)}) all-reduce(f32[]{:T(128)} %get-tuple-element.24, f32[]{:T(128)} %get-tuple-element.25), channel_id=1, replica_groups=mesh['px_0'=2,'px_1'=4,'px_2'=2,'py_0'=4,'py_1'=8] {'py_1'}, use_global_device_ids=true, to_apply=%region_7.8 | all-reduce | flops 2 | bytes 16 | tf_op jit(solution)/shard_map/psum | solution.py:37
  205.1 0.9 copy-done.3
  206.4 1.7 fusion
  208.1 0.7 add.365
  208.9 0.9 copy-done.21
  211.5 6.9 %collective-permute-start.10 = (f32[1,24,128]{2,1,0:T(8,128)S(1)}, f32[1,24,128]{2,1,0:T(8,128)S(1)}, u32[]{:S(2)}, u32[]{:S(2)}) collective-permute-start(f32[1,24,128]{2,1,0:T(8,128)S(1)} %pad_add_fusion.8), channel_id=1, source_target_pairs={{0,32},{32,64},{64,96},{96,128},{128,160},{160,192},{192,224},{224... | collective-permute-start | bytes 36872 | tf_op jit(solution)/shard_map/ppermute | solution.py:27
  218.4 3.6 %collective-permute-start.11 = (f32[40,24,1]{2,1,0:T(8,128)S(1)}, f32[40,24,1]{2,1,0:T(8,128)S(1)}, u32[]{:S(2)}, u32[]{:S(2)}) collective-permute-start(f32[40,24,1]{2,1,0:T(8,128)S(1)} %fusion.10), channel_id=1, source_target_pairs={{0,1},{1,2},{2,3},{3,4},{4,5},{5,6},{6,7},{7,8},{8,9},{9,10},{10,1... | collective-permute-start | bytes 11528 | tf_op jit(solution)/shard_map/ppermute | solution.py:27
  222.0 0.9 multiply_reduce_fusion
  223.0 13.9 %collective-permute-done.11 = f32[40,24,1]{2,1,0:T(8,128)S(1)} collective-permute-done((f32[40,24,1]{2,1,0:T(8,128)S(1)}, f32[40,24,1]{2,1,0:T(8,128)S(1)}, u32[]{:S(2)}, u32[]{:S(2)}) %collective-permute-start.11) | collective-permute-done | bytes 3872 | tf_op jit(solution)/shard_map/ppermute | solution.py:27
  237.0 0.8 fusion.21
  237.9 0.8 fusion.20
  242.4 15.4 %all-reduce.26 = (f32[]{:T(128)}, f32[]{:T(128)}) all-reduce(f32[]{:T(128)S(6)} %add.371, f32[]{:T(128)S(6)} %add.389), channel_id=1, replica_groups=mesh['px_0'=2,'px_1'=4,'px_2'=2,'py_0'=4,'py_1'=8] {'px_0'}, use_global_device_ids=true, to_apply=%region_19.20 | all-reduce | flops 2 | bytes 16 | tf_op jit(solution)/shard_map/psum | solution.py:37
  257.7 7.3 %all-reduce.22 = (f32[]{:T(128)}, f32[]{:T(128)}) all-reduce(f32[]{:T(128)} %get-tuple-element.34, f32[]{:T(128)} %get-tuple-element.35), channel_id=1, replica_groups=mesh['px_0'=2,'px_1'=4,'px_2'=2,'py_0'=4,'py_1'=8] {'px_1'}, use_global_device_ids=true, to_apply=%region_20.21 | all-reduce | flops 2 | bytes 16 | tf_op jit(solution)/shard_map/psum | solution.py:37
  265.0 6.0 %all-reduce.24 = (f32[]{:T(128)}, f32[]{:T(128)}) all-reduce(f32[]{:T(128)} %get-tuple-element.26, f32[]{:T(128)} %get-tuple-element.27), channel_id=1, replica_groups=mesh['px_0'=2,'px_1'=4,'px_2'=2,'py_0'=4,'py_1'=8] {'px_2'}, use_global_device_ids=true, to_apply=%region_21.22 | all-reduce | flops 2 | bytes 16 | tf_op jit(solution)/shard_map/psum | solution.py:37
  271.0 8.8 %all-reduce.20 = (f32[]{:T(128)}, f32[]{:T(128)}) all-reduce(f32[]{:T(128)} %get-tuple-element.30, f32[]{:T(128)} %get-tuple-element.31), channel_id=1, replica_groups=mesh['px_0'=2,'px_1'=4,'px_2'=2,'py_0'=4,'py_1'=8] {'py_0'}, use_global_device_ids=true, to_apply=%region_22.23 | all-reduce | flops 2 | bytes 16 | tf_op jit(solution)/shard_map/psum | solution.py:37
  279.9 11.3 %all-reduce.18 = (f32[]{:T(128)}, f32[]{:T(128)}) all-reduce(f32[]{:T(128)} %get-tuple-element.22, f32[]{:T(128)} %get-tuple-element.23), channel_id=1, replica_groups=mesh['px_0'=2,'px_1'=4,'px_2'=2,'py_0'=4,'py_1'=8] {'py_1'}, use_global_device_ids=true, to_apply=%region_23.24 | all-reduce | flops 2 | bytes 16 | tf_op jit(solution)/shard_map/psum | solution.py:37
  295.7 2.1 multiply_add_fusion
  298.0 0.9 copy-done.24
  299.1 1.1 copy.14
  300.2 1.6 fusion.3
  (110 shorter events, 8.8 us)
Async XLA Ops:
  1.3 37.7 %collective-permute-start = (f32[1,24,128]{2,1,0:T(8,128)S(1)}, f32[1,24,128]{2,1,0:T(8,128)S(1)}, u32[]{:S(2)}, u32[]{:S(2)}) collective-permute-start(f32[1,24,128]{2,1,0:T(8,128)S(1)} %slice.163), channel_id=1, source_target_pairs={{0,480},{32,0},{64,32},{96,64},{128,96},{160,128},{192,160},{224,1... | collective-permute-start | bytes 36872 | tf_op jit(solution)/shard_map/ppermute | solution.py:17
  10.1 10.2 %copy-start.34 = (s32[40,128]{1,0:T(8,128)S(1)}, s32[40,128]{1,0:T(8,128)}, u32[]{:S(2)}) copy-start(s32[40,128]{1,0:T(8,128)} %param.10) | copy-start | bytes 61444
  10.1 10.3 %copy-start.13 = (f32[40,24,128]{2,1,0:T(8,128)S(1)}, f32[40,24,128]{2,1,0:T(8,128)}, u32[]{:S(2)}) copy-start(f32[40,24,128]{2,1,0:T(8,128)} %param.12) | copy-start | bytes 1474564
  10.1 28.9 %collective-permute-start.1 = (f32[40,24,1]{2,1,0:T(8,128)}, f32[40,24,1]{2,1,0:T(8,128)S(1)}, u32[]{:S(2)}, u32[]{:S(2)}) collective-permute-start(f32[40,24,1]{2,1,0:T(8,128)} %bitcast.144), channel_id=1, source_target_pairs={{0,31},{1,0},{2,1},{3,2},{4,3},{5,4},{6,5},{7,6},{8,7},{9,8},{10,9... | collective-permute-start | bytes 11528 | tf_op jit(solution)/shard_map/ppermute | solution.py:17
  20.3 1.0 copy-start.23
  21.4 17.7 %copy-start.12 = (f32[40,24,128]{2,1,0:T(8,128)S(1)}, f32[40,24,128]{2,1,0:T(8,128)}, u32[]{:S(2)}) copy-start(f32[40,24,128]{2,1,0:T(8,128)} %param.11) | copy-start | bytes 1474564
  21.4 17.7 %copy-start.25 = (bf16[40,24,128]{2,1,0:T(8,128)(2,1)S(1)}, bf16[40,24,128]{2,1,0:T(8,128)(2,1)}, u32[]{:S(2)}) copy-start(bf16[40,24,128]{2,1,0:T(8,128)(2,1)} %param.9) | copy-start | bytes 737284
  21.5 17.6 %copy-start = (bf16[3,40,24,128]{3,2,1,0:T(8,128)(2,1)S(1)}, bf16[3,40,24,128]{3,2,1,0:T(8,128)(2,1)}, u32[]{:S(2)}) copy-start(bf16[3,40,24,128]{3,2,1,0:T(8,128)(2,1)} %param.7) | copy-start | bytes 2211844
  21.5 17.6 %copy-start.20 = (bf16[40,24,128]{2,1,0:T(8,128)(2,1)S(1)}, bf16[40,24,128]{2,1,0:T(8,128)(2,1)}, u32[]{:S(2)}) copy-start(bf16[40,24,128]{2,1,0:T(8,128)(2,1)} %param.8) | copy-start | bytes 737284
  39.0 1.6 copy-start.11
  39.1 0.9 copy-start.6
  40.7 43.1 %collective-permute-start.2 = (f32[1,24,128]{2,1,0:T(8,128)S(1)}, f32[1,24,128]{2,1,0:T(8,128)S(1)}, u32[]{:S(2)}, u32[]{:S(2)}) collective-permute-start(f32[1,24,128]{2,1,0:T(8,128)S(1)} %pad_add_fusion.11), channel_id=1, source_target_pairs={{0,32},{32,64},{64,96},{96,128},{128,160},{160,192},{192,224},{224... | collective-permute-start | bytes 36872 | tf_op jit(solution)/shard_map/ppermute | solution.py:27
  46.5 22.8 %collective-permute-start.4 = (f32[40,24,1]{2,1,0:T(8,128)S(1)}, f32[40,24,1]{2,1,0:T(8,128)S(1)}, u32[]{:S(2)}, u32[]{:S(2)}) collective-permute-start(f32[40,24,1]{2,1,0:T(8,128)S(1)} %fusion.6), channel_id=1, source_target_pairs={{0,1},{1,2},{2,3},{3,4},{4,5},{5,6},{6,7},{7,8},{8,9},{9,10},{10,1... | collective-permute-start | bytes 11528 | tf_op jit(solution)/shard_map/ppermute | solution.py:27
  49.4 37.6 %copy-start.2 = (f32[40,24,127]{2,1,0:T(8,128)}, f32[40,24,127]{2,1,0:T(8,128)S(1)}, u32[]{:S(2)}) copy-start(f32[40,24,127]{2,1,0:T(8,128)S(1)} %pad_add_fusion.4) | copy-start | bytes 1463044
  69.5 135.6 %copy-start.1 = (f32[40,24,1]{2,1,0:T(8,128)}, f32[40,24,1]{2,1,0:T(8,128)S(1)}, u32[]{:S(2)}) copy-start(f32[40,24,1]{2,1,0:T(8,128)S(1)} %get-tuple-element.49) | copy-start | bytes 11524
  69.5 14.2 %collective-permute-start.5 = (f32[40,24,1]{2,1,0:T(8,128)S(1)}, f32[40,24,1]{2,1,0:T(8,128)S(1)}, u32[]{:S(2)}, u32[]{:S(2)}) collective-permute-start(f32[40,24,1]{2,1,0:T(8,128)S(1)} %get-tuple-element.50), channel_id=1, source_target_pairs={{1,0},{2,1},{3,2},{4,3},{5,4},{6,5},{7,6},{8,7},{9,8},{10,9},{11,1... | collective-permute-start | bytes 11528 | tf_op jit(solution)/shard_map/ppermute | solution.py:29
  71.5 18.0 %copy-start.8 = (f32[39,24,128]{2,1,0:T(8,128)}, f32[39,24,128]{2,1,0:T(8,128)S(1)}, u32[]{:S(2)}) copy-start(f32[39,24,128]{2,1,0:T(8,128)S(1)} %pad_add_fusion.7) | copy-start | bytes 1437700
  83.8 3.6 %copy-start.4 = (f32[40,24,1]{2,1,0:T(8,128)}, f32[40,24,1]{2,1,0:T(8,128)S(1)}, u32[]{:S(2)}) copy-start(f32[40,24,1]{2,1,0:T(8,128)S(1)} %add.340) | copy-start | bytes 11524
  83.8 5.7 %collective-permute-start.3 = (f32[1,24,128]{2,1,0:T(8,128)S(1)}, f32[1,24,128]{2,1,0:T(8,128)S(1)}, u32[]{:S(2)}, u32[]{:S(2)}) collective-permute-start(f32[1,24,128]{2,1,0:T(8,128)S(1)} %get-tuple-element.54), channel_id=1, source_target_pairs={{32,0},{64,32},{96,64},{128,96},{160,128},{192,160},{224,192},{256... | collective-permute-start | bytes 36872 | tf_op jit(solution)/shard_map/ppermute | solution.py:29
  89.5 0.6 copy-start.27
  91.4 2.2 copy-start.32
  91.5 31.8 %collective-permute-start.6 = (f32[1,24,128]{2,1,0:T(8,128)S(1)}, f32[1,24,128]{2,1,0:T(8,128)S(1)}, u32[]{:S(2)}, u32[]{:S(2)}) collective-permute-start(f32[1,24,128]{2,1,0:T(8,128)S(1)} %pad_add_fusion.9), channel_id=1, source_target_pairs={{0,32},{32,64},{64,96},{96,128},{128,160},{160,192},{192,224},{224... | collective-permute-start | bytes 36872 | tf_op jit(solution)/shard_map/ppermute | solution.py:27
  93.6 12.0 %collective-permute-start.9 = (f32[40,24,1]{2,1,0:T(8,128)S(1)}, f32[40,24,1]{2,1,0:T(8,128)S(1)}, u32[]{:S(2)}, u32[]{:S(2)}) collective-permute-start(f32[40,24,1]{2,1,0:T(8,128)S(1)} %fusion.9), channel_id=1, source_target_pairs={{1,0},{2,1},{3,2},{4,3},{5,4},{6,5},{7,6},{8,7},{9,8},{10,9},{11,1... | collective-permute-start | bytes 11528 | tf_op jit(solution)/shard_map/ppermute | solution.py:29
  100.8 21.5 %copy-start.14 = (f32[40,24,127]{2,1,0:T(8,128)}, f32[40,24,127]{2,1,0:T(8,128)S(1)}, u32[]{:S(2)}) copy-start(f32[40,24,127]{2,1,0:T(8,128)S(1)} %pad_add_fusion.3) | copy-start | bytes 1463044
  106.6 15.7 %collective-permute-start.7 = (f32[40,24,1]{2,1,0:T(8,128)S(1)}, f32[40,24,1]{2,1,0:T(8,128)S(1)}, u32[]{:S(2)}, u32[]{:S(2)}) collective-permute-start(f32[40,24,1]{2,1,0:T(8,128)S(1)} %get-tuple-element.44), channel_id=1, source_target_pairs={{0,1},{1,2},{2,3},{3,4},{4,5},{5,6},{6,7},{7,8},{8,9},{9,10},{10,1... | collective-permute-start | bytes 11528 | tf_op jit(solution)/shard_map/ppermute | solution.py:27
  108.6 15.3 %copy-start.18 = (f32[39,24,128]{2,1,0:T(8,128)}, f32[39,24,128]{2,1,0:T(8,128)S(1)}, u32[]{:S(2)}) copy-start(f32[39,24,128]{2,1,0:T(8,128)S(1)} %pad_add_fusion.6) | copy-start | bytes 1437700
  122.4 0.9 copy-start.16
  123.9 0.8 copy-start.30
  128.5 79.6 %collective-permute-start.8 = (f32[1,24,128]{2,1,0:T(8,128)}, f32[1,24,128]{2,1,0:T(8,128)}, u32[]{:S(2)}, u32[]{:S(2)}) collective-permute-start(f32[1,24,128]{2,1,0:T(8,128)} %get-tuple-element.48), channel_id=1, source_target_pairs={{32,0},{64,32},{96,64},{128,96},{160,128},{192,160},{224,192},{256... | collective-permute-start | bytes 36872 | tf_op jit(solution)/shard_map/ppermute | solution.py:29
  204.9 1.0 copy-start.3
  204.9 1.2 copy-start.5
  204.9 1.3 copy-start.15
  204.9 1.4 copy-start.17
  206.4 1.7 copy-start.33
  206.4 2.5 copy-start.9
  206.4 2.5 copy-start.19
  208.1 0.8 copy-start.28
  208.1 0.8 copy-start.31
  208.9 0.9 copy-start.21
  211.5 26.3 %collective-permute-start.10 = (f32[1,24,128]{2,1,0:T(8,128)S(1)}, f32[1,24,128]{2,1,0:T(8,128)S(1)}, u32[]{:S(2)}, u32[]{:S(2)}) collective-permute-start(f32[1,24,128]{2,1,0:T(8,128)S(1)} %pad_add_fusion.8), channel_id=1, source_target_pairs={{0,32},{32,64},{64,96},{96,128},{128,160},{160,192},{192,224},{224... | collective-permute-start | bytes 36872 | tf_op jit(solution)/shard_map/ppermute | solution.py:27
  218.4 18.4 %collective-permute-start.11 = (f32[40,24,1]{2,1,0:T(8,128)S(1)}, f32[40,24,1]{2,1,0:T(8,128)S(1)}, u32[]{:S(2)}, u32[]{:S(2)}) collective-permute-start(f32[40,24,1]{2,1,0:T(8,128)S(1)} %fusion.10), channel_id=1, source_target_pairs={{0,1},{1,2},{2,3},{3,4},{4,5},{5,6},{6,7},{7,8},{8,9},{9,10},{10,1... | collective-permute-start | bytes 11528 | tf_op jit(solution)/shard_map/ppermute | solution.py:27
  295.7 2.1 copy-start.7
  295.7 2.1 copy-start.10
  295.7 2.1 copy-start.29
  297.8 1.0 copy-start.24
  299.1 1.1 copy-start.22
  299.1 1.1 copy-start.26
where the time goes:
time: 308 us; the launch traced here: 302 us
  blocking collectives  104 us (34%)
  waiting for transfers between devices  84 us (27%)
  starting transfers between devices  70.8 us (23%)
  other arithmetic  20.3 us (7%)
  between operations  14.7 us (5%)
  local copies, waits for them, and re-layouts  7.97 us (3%)
    psum x10, blocking collectives, one_axis_at_a_time(): return functools.reduce(lax.psum, axes, x)  104 us
    ppermute x6, waiting for transfers between devices, extended(): lax.ppermute(tail, axis, [(i, (i + 1) % count) for i in range(count)])  47.5 us
    ppermute x4, starting transfers between devices, extended(): lax.ppermute(head, axis, [((i + 1) % count, i) for i in range(count)])  31.1 us
    ppermute x6, starting transfers between devices, extended(): lax.ppermute(tail, axis, [(i, (i + 1) % count) for i in range(count)])  21.8 us
    ppermute x4, waiting for transfers between devices, extended(): lax.ppermute(head, axis, [((i + 1) % count, i) for i in range(count)])  19.1 us
    ppermute x2, starting transfers between devices, shifted(): lax.ppermute(x, axis, [(i, (i + by) % devices) for i in range(devices)])  17.9 us
    ppermute x2, waiting for transfers between devices, shifted(): lax.ppermute(x, axis, [(i, (i + by) % devices) for i in range(devices)])  17.4 us
    unnamed x74, local copies, waits for them, and re-layouts  7.22 us
  transfers between devices with their start and end apart: 12, of which 7 were waited for; matrix products, arithmetic and copies ran while one was open for 3% of the time, Pallas kernels for 0%

commit v1 on v0

v1 whole, which is shorter than its diff:
```python
import functools
import itertools

import jax
import jax.numpy as jnp
from jax import lax
from jax.experimental import pallas as pl
from jax.experimental.pallas import tpu as pltpu
from jax.sharding import PartitionSpec as P

MESH = pl.DeviceIdType.MESH
F32 = jnp.float32


def factors(px, py):
    if px == 16 and py == 32:
        return (2, 4, 2), (4, 8)
    return (1, px // 2, 2), (2, py // 2)


def peers(px, py, me_x, me_y, dims):
    (ny_lo, nx, nc), (ny_hi, nz) = factors(px, py)
    sizes = {"y_lo": ny_lo, "x": nx, "core": nc, "y_hi": ny_hi, "z": nz}
    here = {
        "core": lax.rem(me_x, nc),
        "x": lax.rem(me_x // nc, nx),
        "y_lo": me_x // (nc * nx),
        "z": lax.rem(me_y, nz),
        "y_hi": me_y // nz,
    }
    found = []
    for offset in itertools.product(*[range(sizes[d]) for d in dims]):
        if not any(offset):
            continue
        there = dict(here)
        for d, o in zip(dims, offset):
            there[d] = lax.rem(here[d] + o, sizes[d])
        found.append(
            {
                "px": (there["y_lo"] * nx + there["x"]) * nc + there["core"],
                "py": there["y_hi"] * nz + there["z"],
            }
        )
    return found


PHASES = (("core", "z"), ("x", "y_lo", "y_hi"))


def group_size(px, py, dims):
    (ny_lo, nx, nc), (ny_hi, nz) = factors(px, py)
    sizes = {"y_lo": ny_lo, "x": nx, "core": nc, "y_hi": ny_hi, "z": nz}
    total = 1
    for d in dims:
        total *= sizes[d]
    return total


def cell(w, e, s, n, b, t, ix, iy, iz, rd, g):
    sx, sy, sz = w + e, s + n, b + t
    total = 3.0 * (ix * sx + iy * sy + iz * sz)
    if g is not None:
        total = total + g
    p = total * rd
    p3 = 3.0 * p
    qx, qy, qz = sx - p3, sy - p3, sz - p3
    return (
        (ix * (qx + w), ix * (qx + e), iy * (qy + s), iy * (qy + n), iz * (qz + b), iz * (qz + t)),
        p,
    )


def halo_kernel(
    px, py,
    metric_h, helm_h, forc_h, orient_h, sx_h, sy_h, sz_h,
    x_ref, y_ref, z_ref, rx, ry, rz, wx, wy, wz, p0, p1, p2, coef,
    metric, helm, forc, orient, ix_s, iy_s, iz_s, rd_s,
    send_b, recv_b, row_b, *rest,
):
    slots = rest[: len(PHASES)]
    load_sem, send_sem, recv_sem, ar_send, ar_recv = rest[len(PHASES) :]
    n, levels, m = helm.shape
    me_x, me_y = lax.axis_index("px"), lax.axis_index("py")
    west = {"px": lax.rem(me_x + px - 1, px), "py": me_y}
    east = {"px": lax.rem(me_x + 1, px), "py": me_y}
    south = {"px": me_x, "py": lax.rem(me_y + py - 1, py)}
    north = {"px": me_x, "py": lax.rem(me_y + 1, py)}
    groups = [peers(px, py, me_x, me_y, dims) for dims in PHASES]

    barrier = pltpu.get_barrier_semaphore()
    greeted = [west, east, south, north] + [d for group in groups for d in group]
    for device in greeted:
        pl.semaphore_signal(barrier, inc=1, device_id=device, device_id_type=MESH)

    loads = [
        pltpu.make_async_copy(src, dst, load_sem.at[k])
        for k, (src, dst) in enumerate(
            [
                (sx_h, x_ref.at[pl.ds(0, n)]),
                (sy_h, y_ref),
                (metric_h, metric),
                (orient_h, orient),
                (helm_h, helm),
                (forc_h, forc),
                (sz_h, z_ref),
            ]
        )
    ]
    for load in loads:
        load.start()

    lane = lax.broadcasted_iota(jnp.int32, (levels, m), 1)
    level = lax.broadcasted_iota(jnp.int32, (levels, m), 0)
    zero = jnp.zeros((levels, m), F32)

    def exchange(k, device):
        return pltpu.make_async_remote_copy(
            src_ref=send_b.at[k],
            dst_ref=recv_b.at[k],
            send_sem=send_sem.at[k],
            recv_sem=recv_sem.at[k],
            device_id=device,
            device_id_type=MESH,
        )

    loads[0].wait()
    loads[1].wait()
    send_b[0] = x_ref[0]

    def pack(i, acc):
        return jnp.where(lane == i, pltpu.roll(y_ref[i], i, 1), acc)

    send_b[1] = lax.fori_loop(0, n, pack, zero, unroll=4)

    pl.semaphore_wait(barrier, len(greeted))
    first = [exchange(0, west), exchange(1, south)]
    for copy in first:
        copy.start()

    for load in loads[2:]:
        load.wait()

    def coefficient(i, carry):
        a = 1.0 / metric[0, i].astype(F32)
        b = 1.0 / metric[1, i].astype(F32)
        c = 1.0 / metric[2, i].astype(F32)
        turned = orient[pl.ds(i, 1), :] == 1
        ix_s[i] = jnp.where(turned, b, a)
        iy_s[i] = jnp.where(turned, a, b)
        iz_s[i] = c
        rd_s[i] = 1.0 / (helm[i].astype(F32) + 6.0 * (a + b + c))
        return carry

    lax.fori_loop(0, n, coefficient, 0, unroll=2)

    def northern(i, s, strip):
        rolled = pltpu.roll(s, m - 1, 1)
        return jnp.where(lane == m - 1, pltpu.roll(strip, m - 1 - i, 1), rolled)

    def to_lane0(i, strip):
        return jnp.where(lane == 0, pltpu.roll(strip, lax.rem(m - i, m), 1), 0.0)

    def vertical(i, ref):
        return ref[pl.ds(i, levels, stride=n), :], ref[pl.ds(i + n, levels, stride=n), :]

    def put_z(i, ref, fb, ft, sign):
        shifted = pltpu.roll(ft, 1, 0)
        body = fb + jnp.where(level == 0, 0.0, shifted)
        ref[pl.ds(i, levels, stride=n), :] = sign * body
        ref[pl.ds(i + levels * n, 1), :] = sign * shifted[0:1]

    def assemble(i, flux, fe_before, strips, outs, sign):
        fw, fe, fs, fn, fb, ft = flux
        out_x, out_y, out_z = outs
        out_x[i] = sign * (fw + fe_before)
        out_y[i] = sign * (fs + jnp.where(lane == 0, 0.0, pltpu.roll(fn, 1, 1)))
        put_z(i, out_z, fb, ft, sign)
        strip_s = jnp.where(lane == i, pltpu.roll(fs, i, 1), strips[0])
        strip_n = jnp.where(lane == i, pltpu.roll(fn, i + 1, 1), strips[1])
        return fe, (strip_s, strip_n)

    def send_partials(base, out_x, fe_last, strips, sign):
        send_b[base] = out_x[0]
        send_b[base + 1] = sign * fe_last
        send_b[base + 2] = sign * strips[0]
        send_b[base + 3] = sign * strips[1]
        copies = [exchange(base + k, d) for k, d in enumerate((west, east, south, north))]
        for copy in copies:
            copy.start()
        return copies

    def receive_partials(base, copies, out_x):
        for copy in copies:
            copy.wait_recv()
        out_x[0] = out_x[0] + recv_b[base + 1]
        out_x[n] = send_b[base + 1] + recv_b[base]
        return recv_b[base + 3], send_b[base + 3] + recv_b[base + 2]

    for copy in first:
        copy.wait_recv()
    x_ref[n] = recv_b[0]
    start_north = recv_b[1]

    def residual(i, carry):
        fe_before, strips = carry
        s = y_ref[i]
        b, t = vertical(i, z_ref)
        flux, p = cell(
            x_ref[i], x_ref[i + 1], s, northern(i, s, start_north), b, t,
            ix_s[i], iy_s[i], iz_s[i], rd_s[i], forc[i].astype(F32),
        )
        p0[i] = p
        return assemble(i, flux, fe_before, strips, (rx, ry, rz), -1.0)

    fe_last, strips = lax.fori_loop(0, n, residual, (zero, (zero, zero)))
    copies1 = send_partials(2, rx, fe_last, strips, -1.0)

    low, high = receive_partials(2, copies1, rx)

    def image(i, carry):
        fe_before, strips, rr = carry
        s = ry[i] + to_lane0(i, low)
        ry[i] = s
        b, t = vertical(i, rz)
        w = rx[i]
        flux, p = cell(
            w, rx[i + 1], s, northern(i, s, high), b, t,
            ix_s[i], iy_s[i], iz_s[i], rd_s[i], None,
        )
        p1[i] = p
        top = jnp.where(level == levels - 1, t, 0.0)
        rr = rr + (w * w + s * s + b * b + top * top)
        fe, strips = assemble(i, flux, fe_before, strips, (wx, wy, wz), 1.0)
        return fe, strips, rr

    fe_last, strips, rr = lax.fori_loop(0, n, image, (zero, (zero, zero), zero))
    copies2 = send_partials(6, wx, fe_last, strips, 1.0)

    low2, high2 = receive_partials(6, copies2, wx)

    def products(i, carry):
        rw, ww, waw = carry
        s = wy[i] + to_lane0(i, low2)
        wy[i] = s
        b, t = vertical(i, wz)
        rb, rt = vertical(i, rz)
        w, e = wx[i], wx[i + 1]
        north_side = northern(i, s, high2)
        flux, p = cell(
            w, e, s, north_side, b, t,
            ix_s[i], iy_s[i], iz_s[i], rd_s[i], None,
        )
        p2[i] = p
        top = jnp.where(level == levels - 1, t, 0.0)
        rw = rw + (w * rx[i] + s * ry[i] + b * rb + top * rt)
        ww = ww + (w * w + s * s + b * b + top * top)
        fw, fe, fs, fn, fb, ft = flux
        waw = waw + ((w * fw + e * fe) + (s * fs + north_side * fn) + (b * fb + t * ft))
        return rw, ww, waw

    rw, ww, waw = lax.fori_loop(0, n, products, (zero, zero, zero))

    lane_row = lax.broadcasted_iota(jnp.int32, (1, m), 1)
    row = jnp.zeros((1, m), F32)
    for k, part in enumerate((rr, rw, ww, waw)):
        whole = jnp.sum(jnp.sum(part, axis=0, keepdims=True), axis=1, keepdims=True)
        row = jnp.where(lane_row == k, whole, row)

    for k, (group, slot) in enumerate(zip(groups, slots)):
        row_b[k] = row
        for j, device in enumerate(group):
            pltpu.make_async_remote_copy(
                src_ref=row_b.at[pl.ds(k, 1)],
                dst_ref=slot.at[pl.ds(j, 1)],
                send_sem=ar_send.at[k],
                recv_sem=ar_recv.at[k],
                device_id=device,
                device_id_type=MESH,
            ).start()
        everything = pltpu.make_async_remote_copy(
            src_ref=slot, dst_ref=slot, send_sem=ar_send.at[k], recv_sem=ar_recv.at[k],
            device_id=group[0], device_id_type=MESH,
        )
        everything.wait_recv()
        row = row + jnp.sum(slot[...], axis=0)
        everything.wait_send()

    sums = [
        jnp.sum(jnp.where(lane_row == k, row, 0.0), axis=1, keepdims=True) for k in range(4)
    ]
    rr, rw, ww, waw = sums
    a0 = rr / rw
    grown = ww * a0 / rw
    b = grown - 1.0
    a1 = b * rr / (a0 * a0 * waw - grown * grown * rw)
    coef[0] = jnp.broadcast_to(a0 + a1 * grown, coef.shape[1:])
    coef[1] = jnp.broadcast_to(-a1 * a0, coef.shape[1:])
    for copy in first + copies1 + copies2:
        copy.wait_send()


def combine_kernel(
    x_ref, y_ref, z_ref, rx, ry, rz, wx, wy, wz, p0, p1, p2, coef,
    ox_h, oy_h, oz_h, op_h, ox, oy, oz, op, sem,
):
    n = ox.shape[0]
    chunks = 5
    rows = n // chunks
    step = n
    c1, c2 = coef[0, 0:1, :], coef[1, 0:1, :]
    copies = []
    for k in range(chunks):

        def body(i, carry):
            ox[i] = x_ref[i] + (c1 * rx[i] + c2 * wx[i])
            oy[i] = y_ref[i] + (c1 * ry[i] + c2 * wy[i])
            op[i] = p0[i] + (c1 * p1[i] + c2 * p2[i])
            return carry

        lax.fori_loop(k * rows, (k + 1) * rows, body, 0)
        tall = oz.shape[0] // chunks

        def body_z(i, carry):
            at = pl.ds(pl.multiple_of(i * step, step), step)
            oz[at, :] = z_ref[at, :] + (c1 * rz[at, :] + c2 * wz[at, :])
            return carry

        lax.fori_loop(k * (tall // step), (k + 1) * (tall // step), body_z, 0)
        span = pl.ds(k * rows, rows)
        span_z = pl.ds(k * tall, tall)
        for j, (src, dst, at) in enumerate(
            ((ox, ox_h, span), (oy, oy_h, span), (oz, oz_h, span_z), (op, op_h, span))
        ):
            copy = pltpu.make_async_copy(src.at[at], dst.at[at], sem.at[k, j])
            copy.start()
            copies.append(copy)
    for copy in copies:
        copy.wait()


def local(px, py, metric, helmholtz, forcing, orientation, start_x, start_y, start_z):
    n, levels, m = helmholtz.shape
    face = (n, levels, m)
    longer = (n + 1, levels, m)
    taller = ((levels + 1) * n, m)
    start_z = jnp.transpose(start_z, (1, 0, 2)).reshape(taller)
    arguments = [
        pltpu.with_memory_space_constraint(a, pltpu.HBM)
        for a in (metric, helmholtz, forcing, orientation, start_x, start_y, start_z)
    ]
    shapes = [longer, face, taller, longer, face, taller, longer, face, taller, face, face, face, (2, 8, m)]
    held = pl.pallas_call(
        functools.partial(halo_kernel, px, py),
        out_shape=[pltpu.VMEM(shape, F32) for shape in shapes],
        in_specs=[pl.BlockSpec(memory_space=pl.ANY)] * 7,
        out_specs=[pl.BlockSpec(memory_space=pltpu.VMEM)] * len(shapes),
        scratch_shapes=[
            pltpu.VMEM((3,) + face, metric.dtype),
            pltpu.VMEM(face, helmholtz.dtype),
            pltpu.VMEM(face, forcing.dtype),
            pltpu.VMEM((n, m), jnp.int32),
            pltpu.VMEM(face, F32),
            pltpu.VMEM(face, F32),
            pltpu.VMEM(face, F32),
            pltpu.VMEM(face, F32),
            pltpu.VMEM((10, levels, m), F32),
            pltpu.VMEM((10, levels, m), F32),
            pltpu.VMEM((len(PHASES), 1, m), F32),
        ]
        + [pltpu.VMEM((group_size(px, py, dims) - 1, 1, m), F32) for dims in PHASES]
        + [
            pltpu.SemaphoreType.DMA((7,)),
            pltpu.SemaphoreType.DMA((10,)),
            pltpu.SemaphoreType.DMA((10,)),
            pltpu.SemaphoreType.DMA((len(PHASES),)),
            pltpu.SemaphoreType.DMA((len(PHASES),)),
        ],
        compiler_params=pltpu.CompilerParams(
            collective_id=0, has_side_effects=True, vmem_limit_bytes=40 * 1024 * 1024
        ),
        name="halo",
    )(*arguments)
    outs = [face, face, taller, face]
    trace_x, trace_y, trace_z, pressure = pl.pallas_call(
        combine_kernel,
        out_shape=[jax.ShapeDtypeStruct(shape, F32) for shape in outs],
        in_specs=[pl.BlockSpec(memory_space=pltpu.VMEM)] * len(shapes),
        out_specs=[pl.BlockSpec(memory_space=pl.ANY)] * 4,
        scratch_shapes=[pltpu.VMEM(shape, F32) for shape in outs]
        + [pltpu.SemaphoreType.DMA((5, 4))],
        compiler_params=pltpu.CompilerParams(vmem_limit_bytes=20 * 1024 * 1024),
        name="combine",
    )(*held)
    trace_z = jnp.transpose(trace_z.reshape(levels + 1, n, m), (1, 0, 2))
    return trace_x, trace_y, trace_z, pressure


def solution(mesh):
    px, py = mesh.shape["px"], mesh.shape["py"]
    columns = P("px", None, "py")
    return jax.shard_map(
        functools.partial(local, px, py),
        mesh=mesh,
        in_specs=(P(None, "px", None, "py"), columns, columns, P("px", "py"), columns, columns, columns),
        out_specs=(columns,) * 4,
        check_vma=False,
    )
```

time: 308 us -> 62.6 us (0.20); the launches traced: 302 us -> 62.5 us
  blocking collectives: 104 us -> 0 us
  waiting for transfers between devices: 84 us -> 0 us
  starting transfers between devices: 70.8 us -> 0 us
  Pallas kernels: 0 us -> 61.9 us
  other arithmetic: 20.3 us -> 0 us
  between operations: 14.7 us -> 0.64 us
  local copies, waits for them, and re-layouts: 7.97 us -> 0 us
    psum x10 -> x0, blocking collectives: 104 us -> none  [one_axis_at_a_time(): return functools.reduce(lax.psum, axes, x)]
    ppermute x12 -> x0, waiting for transfers between devices: 84 us -> none  [the longest x6 47.5 us: extended(): lax.ppermute(tail, axis, [(i, (i + 1) % count) for i in range(count)])]
    ppermute x12 -> x0, starting transfers between devices: 70.8 us -> none  [the longest x4 31.1 us: extended(): lax.ppermute(head, axis, [((i + 1) % count, i) for i in range(count)])]
    pallas_call x0 -> x2, Pallas kernels: none -> 61.9 us  [the longest x1 60.3 us: local(): pl.pallas_call(functools.partial(halo_kernel, px, py), out_shape=[pltpu.V...]
    add x25 -> x0, other arithmetic: 8.43 us -> none  [the longest x6 4.31 us: combine(): member + scale * other]
    unnamed x74 -> x0, local copies, waits for them, and re-layouts: 7.22 us -> none
    reduce_sum x7 -> x0, other arithmetic: 5.87 us -> none  [the longest x3 2.58 us: shared_inner(): return part_x + part_y + jnp.sum(first_vec[2] * second_vec[2])]
    sub x8 -> x0, other arithmetic: 3.97 us -> none  [the longest x2 1.27 us: element(): inverse_z * (2.0 * trace_bottom + trace_top) - weight_z * pressure]
  transfers between devices with their start and end apart: 12 -> 0, of which waited for: 7 -> 0; matrix products, arithmetic and copies ran while one was open for 3% -> 0% of each run, Pallas kernels for 0% -> 0%
where the time goes in v1:
time: 62.6 us; the launch traced here: 62.5 us
  Pallas kernels  61.9 us (99%)
  between operations  0.64 us (1%)
    pallas_call x1, Pallas kernels, local(): pl.pallas_call(functools.partial(halo_kernel, px, py), out_shape=[pltpu.V...  60.3 us
    pallas_call x1, Pallas kernels, local(): pl.pallas_call(combine_kernel, out_shape=[jax.ShapeDtypeStruct(shape, F32...  1.56 us

profile of v1, /device:TPU:1, one launch (start us, length us, event | category | flops | bytes accessed | tf_op | source)
XLA Modules:
  0.0 62.5 jit_solution(1902593970751105194)
XLA Ops:
  0.6 60.3 %halo.1 = (f32[41,24,128]{2,1,0:T(8,128)S(1)}, f32[40,24,128]{2,1,0:T(8,128)S(1)}, f32[1000,128]{1,0:T(8,128)S(1)}, f32[41,24,128]{2,1,0:T(8,128)S(1)}, f32[40,2...) custom-call(bf16[3,40,24,128]{3,2,1,0:T(8,128)(2,1)} %metric_h.1, ...), custom_call_target="tpu_custom_call" | custom-call | tf_op jit(solution)/shard_map/halo/pallas_call | solution.py:352
  60.9 1.6 %combine.1 = (f32[40,24,128]{2,1,0:T(8,128)}, f32[40,24,128]{2,1,0:T(8,128)}, f32[1000,128]{1,0:T(8,128)}, f32[40,24,128]{2,1,0:T(8,128)}) custom-call(f32[41,24,128]{2,1,0:T(8,128)S(1)} %get-tuple-element.21.x_ref, f32[40,24,128]{2,1,0:T(8,128)S(1)} %get-tuple-element.22.y_ref, f32[1000,128]{1,0:T(8,128)S(1)} %get-tuple-element.23.z_ref, ...), custom_call_target="tpu_custom_call" | custom-call | tf_op jit(solution)/shard_map/combine/pallas_call | solution.py:384

commit v2 on v1

--- a/solution.py
+++ b/solution.py
@@ -28,8 +28,14 @@
         "z": lax.rem(me_y, nz),
         "y_hi": me_y // nz,
     }
+    reach = {"core": 0, "x": 1, "y_lo": 1, "z": 1, "y_hi": 2}
+
+    def far(offset):
+        return sum(reach[d] * min(o, sizes[d] - o) for d, o in zip(dims, offset))
+
     found = []
-    for offset in itertools.product(*[range(sizes[d]) for d in dims]):
+    offsets = itertools.product(*[range(sizes[d]) for d in dims])
+    for offset in sorted(offsets, key=far, reverse=True):
         if not any(offset):
             continue
         there = dict(here)
@@ -151,7 +157,7 @@
         rd_s[i] = 1.0 / (helm[i].astype(F32) + 6.0 * (a + b + c))
         return carry
 
-    lax.fori_loop(0, n, coefficient, 0, unroll=2)
+    lax.fori_loop(0, n, coefficient, 0, unroll=4)
 
     def northern(i, s, strip):
         rolled = pltpu.roll(s, m - 1, 1)
@@ -212,7 +218,7 @@
         p0[i] = p
         return assemble(i, flux, fe_before, strips, (rx, ry, rz), -1.0)
 
-    fe_last, strips = lax.fori_loop(0, n, residual, (zero, (zero, zero)))
+    fe_last, strips = lax.fori_loop(0, n, residual, (zero, (zero, zero)), unroll=8)
     copies1 = send_partials(2, rx, fe_last, strips, -1.0)
 
     low, high = receive_partials(2, copies1, rx)
@@ -233,7 +239,7 @@
         fe, strips = assemble(i, flux, fe_before, strips, (wx, wy, wz), 1.0)
         return fe, strips, rr
 
-    fe_last, strips, rr = lax.fori_loop(0, n, image, (zero, (zero, zero), zero))
+    fe_last, strips, rr = lax.fori_loop(0, n, image, (zero, (zero, zero), zero), unroll=8)
     copies2 = send_partials(6, wx, fe_last, strips, 1.0)
 
     low2, high2 = receive_partials(6, copies2, wx)
@@ -258,7 +264,7 @@
         waw = waw + ((w * fw + e * fe) + (s * fs + north_side * fn) + (b * fb + t * ft))
         return rw, ww, waw
 
-    rw, ww, waw = lax.fori_loop(0, n, products, (zero, zero, zero))
+    rw, ww, waw = lax.fori_loop(0, n, products, (zero, zero, zero), unroll=8)
 
     lane_row = lax.broadcasted_iota(jnp.int32, (1, m), 1)
     row = jnp.zeros((1, m), F32)

time: 62.6 us -> 45.3 us (0.72)
  Pallas kernels: 61.9 us -> 44.5 us
    pallas_call x1, Pallas kernels: 60.3 us -> 42.9 us  [local(): pl.pallas_call(functools.partial(halo_kernel, px, py), out_shape=[pltpu.V...]
where the time goes in v2:
time: 45.3 us; the launch traced here: 45.1 us
  Pallas kernels  44.5 us (98%)
  between operations  0.64 us (1%)
    pallas_call x1, Pallas kernels, local(): pl.pallas_call(functools.partial(halo_kernel, px, py), out_shape=[pltpu.V...  42.9 us
    pallas_call x1, Pallas kernels, local(): pl.pallas_call(combine_kernel, out_shape=[jax.ShapeDtypeStruct(shape, F32...  1.56 us

profile of v2, /device:TPU:1, one launch (start us, length us, event | category | flops | bytes accessed | tf_op | source)
XLA Modules:
  0.0 45.1 jit_solution(13856989863184528841)
XLA Ops:
  0.6 42.9 %halo.1 = (f32[41,24,128]{2,1,0:T(8,128)S(1)}, f32[40,24,128]{2,1,0:T(8,128)S(1)}, f32[1000,128]{1,0:T(8,128)S(1)}, f32[41,24,128]{2,1,0:T(8,128)S(1)}, f32[40,2...) custom-call(bf16[3,40,24,128]{3,2,1,0:T(8,128)(2,1)} %metric_h.1, ...), custom_call_target="tpu_custom_call" | custom-call | tf_op jit(solution)/shard_map/halo/pallas_call | solution.py:358
  43.6 1.6 %combine.1 = (f32[40,24,128]{2,1,0:T(8,128)}, f32[40,24,128]{2,1,0:T(8,128)}, f32[1000,128]{1,0:T(8,128)}, f32[40,24,128]{2,1,0:T(8,128)}) custom-call(f32[41,24,128]{2,1,0:T(8,128)S(1)} %get-tuple-element.21.x_ref, f32[40,24,128]{2,1,0:T(8,128)S(1)} %get-tuple-element.22.y_ref, f32[1000,128]{1,0:T(8,128)S(1)} %get-tuple-element.23.z_ref, ...), custom_call_target="tpu_custom_call" | custom-call | tf_op jit(solution)/shard_map/combine/pallas_call | solution.py:390

commit v3 on v2

--- a/solution.py
+++ b/solution.py
@@ -81,7 +81,7 @@
     metric_h, helm_h, forc_h, orient_h, sx_h, sy_h, sz_h,
     x_ref, y_ref, z_ref, rx, ry, rz, wx, wy, wz, p0, p1, p2, coef,
     metric, helm, forc, orient, ix_s, iy_s, iz_s, rd_s,
-    send_b, recv_b, row_b, *rest,
+    z_x, rz_x, wz_x, tb, send_b, recv_b, row_b, *rest,
 ):
     slots = rest[: len(PHASES)]
     load_sem, send_sem, recv_sem, ar_send, ar_recv = rest[len(PHASES) :]
@@ -93,17 +93,12 @@
     north = {"px": me_x, "py": lax.rem(me_y + 1, py)}
     groups = [peers(px, py, me_x, me_y, dims) for dims in PHASES]
 
-    barrier = pltpu.get_barrier_semaphore()
-    greeted = [west, east, south, north] + [d for group in groups for d in group]
-    for device in greeted:
-        pl.semaphore_signal(barrier, inc=1, device_id=device, device_id_type=MESH)
-
     loads = [
         pltpu.make_async_copy(src, dst, load_sem.at[k])
         for k, (src, dst) in enumerate(
             [
+                (sy_h, y_ref),
                 (sx_h, x_ref.at[pl.ds(0, n)]),
-                (sy_h, y_ref),
                 (metric_h, metric),
                 (orient_h, orient),
                 (helm_h, helm),
@@ -115,16 +110,29 @@
     for load in loads:
         load.start()
 
+    barrier = pltpu.get_barrier_semaphore()
+    greeted = [west, east, south, north] + [d for group in groups for d in group]
+    for device in greeted:
+        pl.semaphore_signal(barrier, inc=1, device_id=device, device_id_type=MESH)
+
     lane = lax.broadcasted_iota(jnp.int32, (levels, m), 1)
     level = lax.broadcasted_iota(jnp.int32, (levels, m), 0)
+    pair = jnp.right_shift(lane, 1)
+    odd = jnp.bitwise_and(lane, 1) == 1
     zero = jnp.zeros((levels, m), F32)
 
-    def exchange(k, device):
+    def into_strip(i, value, strip):
+        return jnp.where(pair == i, pltpu.roll(value, 2 * i + 1, 1), strip)
+
+    def lane1_into_strip(i, value, strip):
+        return jnp.where(lane == 2 * i + 1, pltpu.roll(value, 2 * i, 1), strip)
+
+    def exchange(source, slot, device):
         return pltpu.make_async_remote_copy(
-            src_ref=send_b.at[k],
-            dst_ref=recv_b.at[k],
-            send_sem=send_sem.at[k],
-            recv_sem=recv_sem.at[k],
+            src_ref=send_b.at[source],
+            dst_ref=recv_b.at[slot],
+            send_sem=send_sem.at[slot],
+            recv_sem=recv_sem.at[slot],
             device_id=device,
             device_id_type=MESH,
         )
@@ -132,148 +140,216 @@
     loads[0].wait()
     loads[1].wait()
     send_b[0] = x_ref[0]
-
-    def pack(i, acc):
-        return jnp.where(lane == i, pltpu.roll(y_ref[i], i, 1), acc)
-
-    send_b[1] = lax.fori_loop(0, n, pack, zero, unroll=4)
+    start_y = lax.fori_loop(0, n, lambda i, acc: into_strip(i, y_ref[i], acc), zero, unroll=20)
+    send_b[1] = start_y
 
     pl.semaphore_wait(barrier, len(greeted))
-    first = [exchange(0, west), exchange(1, south)]
+    first = [exchange(0, 0, west), exchange(1, 1, south)]
     for copy in first:
         copy.start()
 
     for load in loads[2:]:
         load.wait()
 
-    def coefficient(i, carry):
+    def coefficient(i, strips):
         a = 1.0 / metric[0, i].astype(F32)
         b = 1.0 / metric[1, i].astype(F32)
         c = 1.0 / metric[2, i].astype(F32)
         turned = orient[pl.ds(i, 1), :] == 1
-        ix_s[i] = jnp.where(turned, b, a)
-        iy_s[i] = jnp.where(turned, a, b)
-        iz_s[i] = c
-        rd_s[i] = 1.0 / (helm[i].astype(F32) + 6.0 * (a + b + c))
-        return carry
-
-    lax.fori_loop(0, n, coefficient, 0, unroll=4)
-
-    def northern(i, s, strip):
-        rolled = pltpu.roll(s, m - 1, 1)
-        return jnp.where(lane == m - 1, pltpu.roll(strip, m - 1 - i, 1), rolled)
-
-    def to_lane0(i, strip):
-        return jnp.where(lane == 0, pltpu.roll(strip, lax.rem(m - i, m), 1), 0.0)
+        values = (
+            jnp.where(turned, b, a),
+            jnp.where(turned, a, b),
+            c,
+            1.0 / (helm[i].astype(F32) + 6.0 * (a + b + c)),
+            forc[i].astype(F32),
+        )
+        ix_s[i], iy_s[i], iz_s[i], rd_s[i], _ = values
+        return tuple(into_strip(i, v, strip) for v, strip in zip(values, strips))
+
+    strips = lax.fori_loop(0, n, coefficient, (zero,) * 5, unroll=8)
+    for k in range(5):
+        tb[k] = strips[k]
 
     def vertical(i, ref):
-        return ref[pl.ds(i, levels, stride=n), :], ref[pl.ds(i + n, levels, stride=n), :]
-
-    def put_z(i, ref, fb, ft, sign):
-        shifted = pltpu.roll(ft, 1, 0)
-        body = fb + jnp.where(level == 0, 0.0, shifted)
-        ref[pl.ds(i, levels, stride=n), :] = sign * body
-        ref[pl.ds(i + levels * n, 1), :] = sign * shifted[0:1]
-
-    def assemble(i, flux, fe_before, strips, outs, sign):
+        return ref[i, pl.ds(0, levels), :], ref[i, pl.ds(1, levels), :]
+
+    def collect(fields):
+        fx, fy, fz = fields
+
+        def body(i, strips):
+            y = fy[i]
+            b, t = vertical(i, fz)
+            return (
+                into_strip(i, fx[i], strips[0]),
+                into_strip(i, y, strips[1]),
+                lane1_into_strip(i, y, strips[2]),
+                into_strip(i, b, strips[3]),
+                into_strip(i, t, strips[4]),
+            )
+
+        strips = lax.fori_loop(0, n, body, (zero,) * 5, unroll=8)
+        for k in range(5):
+            tb[5 + k] = strips[k]
+
+    def row(i, fields, strip, fresh, source):
+        fx, fy, fz = fields
+        edge = pltpu.roll(strip, m - 1 - 2 * i, 1)
+        s = fy[i]
+        if not fresh:
+            s = s + jnp.where(lane == 0, edge, 0.0)
+        north_side = jnp.where(lane == m - 1, edge, pltpu.roll(s, m - 1, 1))
+        b, t = vertical(i, fz)
+        w, e = fx[i], fx[i + 1]
+        g = forc[i].astype(F32) if source else None
+        flux, p = cell(w, e, s, north_side, b, t, ix_s[i], iy_s[i], iz_s[i], rd_s[i], g)
+        return (w, e, s, north_side, b, t), flux, p
+
+    def send_boundary(base, fields, strip, fresh, source, sign):
+        fx = fields[0]
+        last = pltpu.roll(fx[n], 2 * n - 1, 1)
+        tw = tb[5]
+        te = jnp.where(pair == n - 1, last, pltpu.roll(tw, m - 2, 1))
+        ts = tb[6]
+        if not fresh:
+            tw = jnp.where(pair == 0, pltpu.roll(fx[0], 1, 1), tw)
+            ts = ts + jnp.where(odd, strip, 0.0)
+            tb[10] = ts
+        tn = jnp.where(odd, tb[7], strip)
+        flux, _ = cell(
+            tw, te, ts, tn, tb[8], tb[9], tb[0], tb[1], tb[2], tb[3], tb[4] if source else None
+        )
+        send_b[base + 2] = sign * jnp.where(odd, flux[2], flux[3])
+        send_b[base] = sign * row(0, fields, strip, fresh, source)[1][0]
+        send_b[base + 1] = sign * row(n - 1, fields, strip, fresh, source)[1][1]
+        copies = [
+            exchange(base + 2, base + 2, south),
+            exchange(base + 2, base + 3, north),
+            exchange(base, base, west),
+            exchange(base + 1, base + 1, east),
+        ]
+        for copy in copies:
+            copy.start()
+        return copies
+
+    def arrive(base, copies, out_x):
+        for copy in copies:
+            copy.wait_recv()
+        out_x[0] = out_x[0] + recv_b[base + 1]
+        out_x[n] = out_x[n] + recv_b[base]
+        high = send_b[base + 2] + pltpu.roll(recv_b[base + 2], m - 1, 1)
+        return jnp.where(odd, pltpu.roll(recv_b[base + 3], 1, 1), high)
+
+    def assemble(i, flux, fe_before, outs, sign):
         fw, fe, fs, fn, fb, ft = flux
         out_x, out_y, out_z = outs
         out_x[i] = sign * (fw + fe_before)
         out_y[i] = sign * (fs + jnp.where(lane == 0, 0.0, pltpu.roll(fn, 1, 1)))
-        put_z(i, out_z, fb, ft, sign)
-        strip_s = jnp.where(lane == i, pltpu.roll(fs, i, 1), strips[0])
-        strip_n = jnp.where(lane == i, pltpu.roll(fn, i + 1, 1), strips[1])
-        return fe, (strip_s, strip_n)
-
-    def send_partials(base, out_x, fe_last, strips, sign):
-        send_b[base] = out_x[0]
-        send_b[base + 1] = sign * fe_last
-        send_b[base + 2] = sign * strips[0]
-        send_b[base + 3] = sign * strips[1]
-        copies = [exchange(base + k, d) for k, d in enumerate((west, east, south, north))]
-        for copy in copies:
-            copy.start()
-        return copies
-
-    def receive_partials(base, copies, out_x):
-        for copy in copies:
-            copy.wait_recv()
-        out_x[0] = out_x[0] + recv_b[base + 1]
-        out_x[n] = send_b[base + 1] + recv_b[base]
-        return recv_b[base + 3], send_b[base + 3] + recv_b[base + 2]
-
+        shifted = pltpu.roll(ft, 1, 0)
+        out_z[i, pl.ds(0, levels), :] = sign * (fb + jnp.where(level == 0, 0.0, shifted))
+        out_z[i, pl.ds(levels, 1), :] = sign * shifted[0:1]
+        return fe
+
+    start = (x_ref, y_ref, z_x)
+    residual = (rx, ry, rz_x)
+    image = (wx, wy, wz_x)
+
+    def turn(i, carry):
+        z_x[i] = z_ref[pl.ds(i, levels + 1, stride=n), :]
+        return carry
+
+    lax.fori_loop(0, n, turn, 0, unroll=4)
+    collect(start)
     for copy in first:
         copy.wait_recv()
     x_ref[n] = recv_b[0]
-    start_north = recv_b[1]
-
-    def residual(i, carry):
-        fe_before, strips = carry
-        s = y_ref[i]
-        b, t = vertical(i, z_ref)
-        flux, p = cell(
-            x_ref[i], x_ref[i + 1], s, northern(i, s, start_north), b, t,
-            ix_s[i], iy_s[i], iz_s[i], rd_s[i], forc[i].astype(F32),
-        )
+    strip = pltpu.roll(recv_b[1], m - 1, 1)
+    copies1 = send_boundary(2, start, strip, True, True, -1.0)
+
+    def pass1(i, fe_before):
+        _, flux, p = row(i, start, strip, True, True)
         p0[i] = p
-        return assemble(i, flux, fe_before, strips, (rx, ry, rz), -1.0)
-
-    fe_last, strips = lax.fori_loop(0, n, residual, (zero, (zero, zero)), unroll=8)
-    copies1 = send_partials(2, rx, fe_last, strips, -1.0)
-
-    low, high = receive_partials(2, copies1, rx)
-
-    def image(i, carry):
-        fe_before, strips, rr = carry
-        s = ry[i] + to_lane0(i, low)
+        return assemble(i, flux, fe_before, residual, -1.0)
+
+    rx[n] = -lax.fori_loop(0, n, pass1, zero, unroll=8)
+    collect(residual)
+
+    strip2 = arrive(2, copies1, rx)
+    copies2 = send_boundary(6, residual, strip2, False, False, 1.0)
+
+    def pass2(i, carry):
+        fe_before, rr = carry
+        (w, e, s, north_side, b, t), flux, p = row(i, residual, strip2, False, False)
         ry[i] = s
-        b, t = vertical(i, rz)
-        w = rx[i]
-        flux, p = cell(
-            w, rx[i + 1], s, northern(i, s, high), b, t,
-            ix_s[i], iy_s[i], iz_s[i], rd_s[i], None,
-        )
         p1[i] = p
         top = jnp.where(level == levels - 1, t, 0.0)
         rr = rr + (w * w + s * s + b * b + top * top)
-        fe, strips = assemble(i, flux, fe_before, strips, (wx, wy, wz), 1.0)
-        return fe, strips, rr
-
-    fe_last, strips, rr = lax.fori_loop(0, n, image, (zero, (zero, zero), zero), unroll=8)
-    copies2 = send_partials(6, wx, fe_last, strips, 1.0)
-
-    low2, high2 = receive_partials(6, copies2, wx)
-
-    def products(i, carry):
+        return assemble(i, flux, fe_before, image, 1.0), rr
+
+    wx[n], rr = lax.fori_loop(0, n, pass2, (zero, zero), unroll=8)
+
+    collect(image)
+
+    inner = jnp.logical_and(lane > 0, lane < m - 1)
+
+    def quadratic(faces, flux):
+        w, e, s, north_side, b, t = faces
+        fw, fe, fs, fn, fb, ft = flux
+        return (w * fw + e * fe) + (s * fs + north_side * fn) + (b * fb + t * ft)
+
+    def pass3(i, carry):
         rw, ww, waw = carry
-        s = wy[i] + to_lane0(i, low2)
-        wy[i] = s
-        b, t = vertical(i, wz)
-        rb, rt = vertical(i, rz)
+        s = wy[i]
+        north_side = pltpu.roll(s, m - 1, 1)
+        b, t = vertical(i, wz_x)
+        rb, rt = vertical(i, rz_x)
         w, e = wx[i], wx[i + 1]
-        north_side = northern(i, s, high2)
-        flux, p = cell(
-            w, e, s, north_side, b, t,
-            ix_s[i], iy_s[i], iz_s[i], rd_s[i], None,
-        )
-        p2[i] = p
+        flux, _ = cell(w, e, s, north_side, b, t, ix_s[i], iy_s[i], iz_s[i], rd_s[i], None)
+        between = jnp.logical_and(i > 0, i < n - 1)
+        sm = jnp.where(lane == 0, 0.0, s)
+        top = jnp.where(level == levels - 1, t, 0.0)
+        rw = rw + jnp.where(between, w * rx[i] + sm * ry[i] + b * rb + top * rt, 0.0)
+        ww = ww + jnp.where(between, w * w + sm * sm + b * b + top * top, 0.0)
+        kept = jnp.logical_and(inner, between)
+        waw = waw + jnp.where(kept, quadratic((w, e, s, north_side, b, t), flux), 0.0)
+        return rw, ww, waw
+
+    rw, ww, waw = lax.fori_loop(0, n, pass3, (zero, zero, zero), unroll=8)
+
+    strip3 = arrive(6, copies2, wx)
+    rest_of = jnp.logical_and(pair > 0, pair < n - 1)
+    tw, ts = tb[5], tb[6] + jnp.where(odd, strip3, 0.0)
+    te, tn = pltpu.roll(tw, m - 2, 1), jnp.where(odd, tb[7], strip3)
+    faces = (tw, te, ts, tn, tb[8], tb[9])
+    flux, _ = cell(*faces, tb[0], tb[1], tb[2], tb[3], None)
+    waw = waw + jnp.where(rest_of, quadratic(faces, flux), 0.0)
+    ts = jnp.where(jnp.logical_and(rest_of, odd), ts, 0.0)
+    ww = ww + ts * ts
+    rw = rw + ts * tb[10]
+    for i in (0, n - 1):
+        faces, flux, _ = row(i, image, strip3, False, False)
+        w, _, s, _, b, t = faces
+        rb, rt = vertical(i, rz_x)
         top = jnp.where(level == levels - 1, t, 0.0)
         rw = rw + (w * rx[i] + s * ry[i] + b * rb + top * rt)
         ww = ww + (w * w + s * s + b * b + top * top)
-        fw, fe, fs, fn, fb, ft = flux
-        waw = waw + ((w * fw + e * fe) + (s * fs + north_side * fn) + (b * fb + t * ft))
-        return rw, ww, waw
-
-    rw, ww, waw = lax.fori_loop(0, n, products, (zero, zero, zero), unroll=8)
+        waw = waw + quadratic(faces, flux)
+
+    def finish(i, carry):
+        faces, _, p = row(i, image, strip3, False, False)
+        wy[i] = faces[2]
+        p2[i] = p
+        rz[pl.ds(i, levels + 1, stride=n), :] = rz_x[i]
+        wz[pl.ds(i, levels + 1, stride=n), :] = wz_x[i]
+        return carry
 
     lane_row = lax.broadcasted_iota(jnp.int32, (1, m), 1)
-    row = jnp.zeros((1, m), F32)
+    sums = jnp.zeros((1, m), F32)
     for k, part in enumerate((rr, rw, ww, waw)):
         whole = jnp.sum(jnp.sum(part, axis=0, keepdims=True), axis=1, keepdims=True)
-        row = jnp.where(lane_row == k, whole, row)
+        sums = jnp.where(lane_row == k, whole, sums)
 
     for k, (group, slot) in enumerate(zip(groups, slots)):
-        row_b[k] = row
+        row_b[k] = sums
         for j, device in enumerate(group):
             pltpu.make_async_remote_copy(
                 src_ref=row_b.at[pl.ds(k, 1)],
@@ -283,18 +359,19 @@
                 device_id=device,
                 device_id_type=MESH,
             ).start()
+        if k == 0:
+            lax.fori_loop(0, n, finish, 0, unroll=4)
         everything = pltpu.make_async_remote_copy(
             src_ref=slot, dst_ref=slot, send_sem=ar_send.at[k], recv_sem=ar_recv.at[k],
             device_id=group[0], device_id_type=MESH,
         )
         everything.wait_recv()
-        row = row + jnp.sum(slot[...], axis=0)
+        sums = sums + jnp.sum(slot[...], axis=0)
         everything.wait_send()
 
-    sums = [
-        jnp.sum(jnp.where(lane_row == k, row, 0.0), axis=1, keepdims=True) for k in range(4)
+    rr, rw, ww, waw = [
+        jnp.sum(jnp.where(lane_row == k, sums, 0.0), axis=1, keepdims=True) for k in range(4)
     ]
-    rr, rw, ww, waw = sums
     a0 = rr / rw
     grown = ww * a0 / rw
     b = grown - 1.0
@@ -369,6 +446,10 @@
             pltpu.VMEM(face, F32),
             pltpu.VMEM(face, F32),
             pltpu.VMEM(face, F32),
+            pltpu.VMEM((n, levels + 1, m), F32),
+            pltpu.VMEM((n, levels + 1, m), F32),
+            pltpu.VMEM((n, levels + 1, m), F32),
+            pltpu.VMEM((11, levels, m), F32),
             pltpu.VMEM((10, levels, m), F32),
             pltpu.VMEM((10, levels, m), F32),
             pltpu.VMEM((len(PHASES), 1, m), F32),

time: 45.3 us -> 41 us (0.905)
  Pallas kernels: 44.5 us -> 40.2 us
    pallas_call x1, Pallas kernels: 42.9 us -> 38.6 us  [local(): pl.pallas_call(functools.partial(halo_kernel, px, py), out_shape=[pltpu.V...]
where the time goes in v3:
time: 41 us; the launch traced here: 40.8 us
  Pallas kernels  40.2 us (98%)
  between operations  0.64 us (2%)
    pallas_call x1, Pallas kernels, local(): pl.pallas_call(functools.partial(halo_kernel, px, py), out_shape=[pltpu.V...  38.6 us
    pallas_call x1, Pallas kernels, local(): pl.pallas_call(combine_kernel, out_shape=[jax.ShapeDtypeStruct(shape, F32...  1.56 us

profile of v3, /device:TPU:1, one launch (start us, length us, event | category | flops | bytes accessed | tf_op | source)
XLA Modules:
  0.0 40.8 jit_solution(12175924497555246521)
XLA Ops:
  0.6 38.6 %halo.1 = (f32[41,24,128]{2,1,0:T(8,128)S(1)}, f32[40,24,128]{2,1,0:T(8,128)S(1)}, f32[1000,128]{1,0:T(8,128)S(1)}, f32[41,24,128]{2,1,0:T(8,128)S(1)}, f32[40,2...) custom-call(bf16[3,40,24,128]{3,2,1,0:T(8,128)(2,1)} %metric_h.1, ...), custom_call_target="tpu_custom_call" | custom-call | tf_op jit(solution)/shard_map/halo/pallas_call | solution.py:435
  39.3 1.6 %combine.1 = (f32[40,24,128]{2,1,0:T(8,128)}, f32[40,24,128]{2,1,0:T(8,128)}, f32[1000,128]{1,0:T(8,128)}, f32[40,24,128]{2,1,0:T(8,128)}) custom-call(f32[41,24,128]{2,1,0:T(8,128)S(1)} %get-tuple-element.21.x_ref, f32[40,24,128]{2,1,0:T(8,128)S(1)} %get-tuple-element.22.y_ref, f32[1000,128]{1,0:T(8,128)S(1)} %get-tuple-element.23.z_ref, ...), custom_call_target="tpu_custom_call" | custom-call | tf_op jit(solution)/shard_map/combine/pallas_call | solution.py:471

commit v4 on v3

--- a/solution.py
+++ b/solution.py
@@ -81,7 +81,7 @@
     metric_h, helm_h, forc_h, orient_h, sx_h, sy_h, sz_h,
     x_ref, y_ref, z_ref, rx, ry, rz, wx, wy, wz, p0, p1, p2, coef,
     metric, helm, forc, orient, ix_s, iy_s, iz_s, rd_s,
-    z_x, rz_x, wz_x, tb, send_b, recv_b, row_b, *rest,
+    z_x, rz_x, wz_x, tb, send_b, recv_b, msg_s, msg_r, dia_s, dia_r, row_b, *rest,
 ):
     slots = rest[: len(PHASES)]
     load_sem, send_sem, recv_sem, ar_send, ar_recv = rest[len(PHASES) :]
@@ -91,6 +91,9 @@
     east = {"px": lax.rem(me_x + 1, px), "py": me_y}
     south = {"px": me_x, "py": lax.rem(me_y + py - 1, py)}
     north = {"px": me_x, "py": lax.rem(me_y + 1, py)}
+    corner = [
+        {"px": x["px"], "py": y["py"]} for x in (east, west) for y in (north, south)
+    ]
     groups = [peers(px, py, me_x, me_y, dims) for dims in PHASES]
 
     loads = [
@@ -111,7 +114,7 @@
         load.start()
 
     barrier = pltpu.get_barrier_semaphore()
-    greeted = [west, east, south, north] + [d for group in groups for d in group]
+    greeted = [west, east, south, north] + corner + [d for group in groups for d in group]
     for device in greeted:
         pl.semaphore_signal(barrier, inc=1, device_id=device, device_id_type=MESH)
 
@@ -127,28 +130,17 @@
     def lane1_into_strip(i, value, strip):
         return jnp.where(lane == 2 * i + 1, pltpu.roll(value, 2 * i, 1), strip)
 
-    def exchange(source, slot, device):
+    def exchange(source, target, slot, device):
         return pltpu.make_async_remote_copy(
-            src_ref=send_b.at[source],
-            dst_ref=recv_b.at[slot],
+            src_ref=source,
+            dst_ref=target,
             send_sem=send_sem.at[slot],
             recv_sem=recv_sem.at[slot],
             device_id=device,
             device_id_type=MESH,
         )
 
-    loads[0].wait()
-    loads[1].wait()
-    send_b[0] = x_ref[0]
-    start_y = lax.fori_loop(0, n, lambda i, acc: into_strip(i, y_ref[i], acc), zero, unroll=20)
-    send_b[1] = start_y
-
-    pl.semaphore_wait(barrier, len(greeted))
-    first = [exchange(0, 0, west), exchange(1, 1, south)]
-    for copy in first:
-        copy.start()
-
-    for load in loads[2:]:
+    for load in loads:
         load.wait()
 
     def coefficient(i, strips):
@@ -173,7 +165,7 @@
     def vertical(i, ref):
         return ref[i, pl.ds(0, levels), :], ref[i, pl.ds(1, levels), :]
 
-    def collect(fields):
+    def collect(fields, base):
         fx, fy, fz = fields
 
         def body(i, strips):
@@ -189,7 +181,7 @@
 
         strips = lax.fori_loop(0, n, body, (zero,) * 5, unroll=8)
         for k in range(5):
-            tb[5 + k] = strips[k]
+            tb[base + k] = strips[k]
 
     def row(i, fields, strip, fresh, source):
         fx, fy, fz = fields
@@ -204,40 +196,13 @@
         flux, p = cell(w, e, s, north_side, b, t, ix_s[i], iy_s[i], iz_s[i], rd_s[i], g)
         return (w, e, s, north_side, b, t), flux, p
 
-    def send_boundary(base, fields, strip, fresh, source, sign):
-        fx = fields[0]
-        last = pltpu.roll(fx[n], 2 * n - 1, 1)
-        tw = tb[5]
-        te = jnp.where(pair == n - 1, last, pltpu.roll(tw, m - 2, 1))
-        ts = tb[6]
-        if not fresh:
-            tw = jnp.where(pair == 0, pltpu.roll(fx[0], 1, 1), tw)
-            ts = ts + jnp.where(odd, strip, 0.0)
-            tb[10] = ts
-        tn = jnp.where(odd, tb[7], strip)
-        flux, _ = cell(
-            tw, te, ts, tn, tb[8], tb[9], tb[0], tb[1], tb[2], tb[3], tb[4] if source else None
-        )
-        send_b[base + 2] = sign * jnp.where(odd, flux[2], flux[3])
-        send_b[base] = sign * row(0, fields, strip, fresh, source)[1][0]
-        send_b[base + 1] = sign * row(n - 1, fields, strip, fresh, source)[1][1]
-        copies = [
-            exchange(base + 2, base + 2, south),
-            exchange(base + 2, base + 3, north),
-            exchange(base, base, west),
-            exchange(base + 1, base + 1, east),
-        ]
-        for copy in copies:
-            copy.start()
-        return copies
-
-    def arrive(base, copies, out_x):
-        for copy in copies:
-            copy.wait_recv()
-        out_x[0] = out_x[0] + recv_b[base + 1]
-        out_x[n] = out_x[n] + recv_b[base]
-        high = send_b[base + 2] + pltpu.roll(recv_b[base + 2], m - 1, 1)
-        return jnp.where(odd, pltpu.roll(recv_b[base + 3], 1, 1), high)
+    def strip_flux(base, last, strip, source):
+        te = jnp.where(pair == n - 1, pltpu.roll(last, 2 * n - 1, 1), pltpu.roll(tb[base], m - 2, 1))
+        tn = jnp.where(odd, tb[base + 2], strip)
+        return cell(
+            tb[base], te, tb[base + 1], tn, tb[base + 3], tb[base + 4],
+            tb[0], tb[1], tb[2], tb[3], tb[4] if source else None,
+        )[0]
 
     def assemble(i, flux, fe_before, outs, sign):
         fw, fe, fs, fn, fb, ft = flux
@@ -258,23 +223,115 @@
         return carry
 
     lax.fori_loop(0, n, turn, 0, unroll=4)
-    collect(start)
+    x_ref[n] = zero
+    collect(start, 5)
+
+    flux = strip_flux(5, zero, zero, True)
+    both = 9.0 * tb[0] * tb[1] * tb[3]
+    msg_s[2, 0] = tb[6]
+    msg_s[2, 1] = -flux[2]
+    msg_s[2, 2] = both
+    msg_s[3, 0] = -flux[3]
+    msg_s[3, 1] = 9.0 * tb[1] * tb[1] * tb[3] - 2.0 * tb[1]
+    msg_s[3, 2] = both
+    msg_s[0, 0] = x_ref[0]
+    msg_s[0, 1] = -row(0, start, zero, True, True)[1][0]
+    msg_s[0, 2] = 9.0 * ix_s[0] * iy_s[0] * rd_s[0]
+    msg_s[1, 0] = -row(n - 1, start, zero, True, True)[1][1]
+    msg_s[1, 1] = 9.0 * ix_s[n - 1] * ix_s[n - 1] * rd_s[n - 1] - 2.0 * ix_s[n - 1]
+    msg_s[1, 2] = 9.0 * ix_s[n - 1] * iy_s[n - 1] * rd_s[n - 1]
+    dia_s[0] = jnp.where(
+        lane == m - 1, pltpu.roll(y_ref[0], m - 1, 1), pltpu.roll(x_ref[0], 2 * n - 1, 1)
+    )
+    dia_s[1] = pltpu.roll(y_ref[n - 1], m - 1, 1)
+    north_east, south_east, north_west, south_west = corner
+    first = [
+        exchange(dia_s.at[0], dia_r.at[0], 8, south_west),
+        exchange(dia_s.at[0], dia_r.at[1], 9, north_west),
+        exchange(dia_s.at[1], dia_r.at[2], 10, south_east),
+    ] + [
+        exchange(msg_s.at[k], msg_r.at[k], 4 + k, device)
+        for k, device in ((2, south), (3, north), (0, west), (1, east))
+    ]
+    pl.semaphore_wait(barrier, len(greeted))
+    for copy in first:
+        copy.start()
+
+    def pass1(i, fe_before):
+        _, flux, _ = row(i, start, zero, True, True)
+        return assemble(i, flux, fe_before, residual, -1.0)
+
+    lax.fori_loop(0, n, pass1, zero, unroll=8)
+    collect(residual, 11)
+
     for copy in first:
         copy.wait_recv()
-    x_ref[n] = recv_b[0]
-    strip = pltpu.roll(recv_b[1], m - 1, 1)
-    copies1 = send_boundary(2, start, strip, True, True, -1.0)
-
-    def pass1(i, fe_before):
-        _, flux, p = row(i, start, strip, True, True)
-        p0[i] = p
-        return assemble(i, flux, fe_before, residual, -1.0)
-
-    rx[n] = -lax.fori_loop(0, n, pass1, zero, unroll=8)
-    collect(residual)
-
-    strip2 = arrive(2, copies1, rx)
-    copies2 = send_boundary(6, residual, strip2, False, False, 1.0)
+    x_ref[n] = msg_r[0, 0]
+    strip1 = pltpu.roll(msg_r[2, 0], m - 1, 1)
+    from_east = msg_r[0, 1] + jnp.where(lane == m - 1, msg_r[0, 2] * dia_r[0], 0.0)
+    from_west = (
+        msg_r[1, 0]
+        + msg_r[1, 1] * x_ref[0]
+        + jnp.where(lane == m - 1, msg_r[1, 2] * dia_r[2], 0.0)
+    )
+    from_north = msg_r[2, 1] + jnp.where(lane == 2 * n - 1, msg_r[2, 2] * dia_r[0], 0.0)
+    from_south = (
+        msg_r[3, 0]
+        + msg_r[3, 1] * pltpu.roll(tb[6], m - 1, 1)
+        + jnp.where(lane == 2 * n - 2, msg_r[3, 2] * dia_r[1], 0.0)
+    )
+    high = pltpu.roll(from_north, m - 1, 1) - strip_flux(5, x_ref[n], strip1, True)[3]
+    strip2 = jnp.where(odd, pltpu.roll(from_south, 1, 1), high)
+
+    own = jnp.where(odd, 0.0, strip1)
+    dp = 3.0 * tb[1] * tb[3] * own
+    dx, dz = 3.0 * tb[0] * dp, 3.0 * tb[2] * dp
+    add_x = dx + pltpu.roll(dx, 2, 1)
+    add_y = 3.0 * tb[1] * dp - tb[1] * own
+    add_b = dz + jnp.where(level == 0, 0.0, pltpu.roll(dz, 1, 0))
+    add_t = dz + jnp.where(level == levels - 1, 0.0, pltpu.roll(dz, levels - 1, 0))
+
+    f0 = row(0, start, strip1, True, True)[1]
+    assemble(0, f0, -from_west, residual, -1.0)
+    assemble(1, row(1, start, strip1, True, True)[1], f0[1], residual, -1.0)
+    before = row(n - 2, start, strip1, True, True)[1][1]
+    fe_last = assemble(n - 1, row(n - 1, start, strip1, True, True)[1], before, residual, -1.0)
+    rx[n] = from_east - fe_last
+    b_last, t_last = vertical(n - 1, rz_x)
+    tb[11] = into_strip(0, rx[0], into_strip(n - 1, rx[n - 1], tb[11] + add_x))
+    tb[12] = into_strip(n - 1, ry[n - 1], tb[12] + add_y) + jnp.where(odd, strip2, 0.0)
+    tb[13] = lane1_into_strip(n - 1, ry[n - 1], tb[13])
+    tb[14] = into_strip(n - 1, b_last, tb[14] + add_b)
+    tb[15] = into_strip(n - 1, t_last, tb[15] + add_t)
+
+    flux = strip_flux(11, rx[n], strip2, False)
+    send_b[2] = jnp.where(odd, flux[2], flux[3])
+    send_b[0] = row(0, residual, strip2, False, False)[1][0]
+    send_b[1] = row(n - 1, residual, strip2, False, False)[1][1]
+    second = [
+        exchange(send_b.at[2], recv_b.at[2], 2, south),
+        exchange(send_b.at[2], recv_b.at[3], 3, north),
+        exchange(send_b.at[0], recv_b.at[0], 0, west),
+        exchange(send_b.at[1], recv_b.at[1], 1, east),
+    ]
+    for copy in second:
+        copy.start()
+
+    rows_left = jnp.logical_and(pair > 1, pair < n - 1)
+    adds = [jnp.where(rows_left, a, 0.0) for a in (add_x, add_y, add_b, add_t)]
+
+    def amend(i, carry):
+        ax, ay, ab, at = [
+            jnp.where(lane == m - 1, pltpu.roll(a, m - 1 - 2 * i, 1), 0.0) for a in adds
+        ]
+        rx[i] = rx[i] + ax
+        ry[i] = ry[i] + ay
+        rz_x[i, pl.ds(0, levels), :] = rz_x[i, pl.ds(0, levels), :] + ab
+        top = pl.ds(levels, 1)
+        rz_x[i, top, :] = rz_x[i, top, :] + at[levels - 1 :]
+        return carry
+
+    lax.fori_loop(0, n, amend, 0, unroll=8)
 
     def pass2(i, carry):
         fe_before, rr = carry
@@ -287,7 +344,7 @@
 
     wx[n], rr = lax.fori_loop(0, n, pass2, (zero, zero), unroll=8)
 
-    collect(image)
+    collect(image, 5)
 
     inner = jnp.logical_and(lane > 0, lane < m - 1)
 
@@ -315,7 +372,12 @@
 
     rw, ww, waw = lax.fori_loop(0, n, pass3, (zero, zero, zero), unroll=8)
 
-    strip3 = arrive(6, copies2, wx)
+    for copy in second:
+        copy.wait_recv()
+    wx[0] = wx[0] + recv_b[1]
+    wx[n] = wx[n] + recv_b[0]
+    high = send_b[2] + pltpu.roll(recv_b[2], m - 1, 1)
+    strip3 = jnp.where(odd, pltpu.roll(recv_b[3], 1, 1), high)
     rest_of = jnp.logical_and(pair > 0, pair < n - 1)
     tw, ts = tb[5], tb[6] + jnp.where(odd, strip3, 0.0)
     te, tn = pltpu.roll(tw, m - 2, 1), jnp.where(odd, tb[7], strip3)
@@ -324,7 +386,7 @@
     waw = waw + jnp.where(rest_of, quadratic(faces, flux), 0.0)
     ts = jnp.where(jnp.logical_and(rest_of, odd), ts, 0.0)
     ww = ww + ts * ts
-    rw = rw + ts * tb[10]
+    rw = rw + ts * tb[12]
     for i in (0, n - 1):
         faces, flux, _ = row(i, image, strip3, False, False)
         w, _, s, _, b, t = faces
@@ -338,6 +400,7 @@
         faces, _, p = row(i, image, strip3, False, False)
         wy[i] = faces[2]
         p2[i] = p
+        p0[i] = row(i, start, strip1, True, True)[2]
         rz[pl.ds(i, levels + 1, stride=n), :] = rz_x[i]
         wz[pl.ds(i, levels + 1, stride=n), :] = wz_x[i]
         return carry
@@ -378,7 +441,7 @@
     a1 = b * rr / (a0 * a0 * waw - grown * grown * rw)
     coef[0] = jnp.broadcast_to(a0 + a1 * grown, coef.shape[1:])
     coef[1] = jnp.broadcast_to(-a1 * a0, coef.shape[1:])
-    for copy in first + copies1 + copies2:
+    for copy in first + second:
         copy.wait_send()
 
 
@@ -449,16 +512,20 @@
             pltpu.VMEM((n, levels + 1, m), F32),
             pltpu.VMEM((n, levels + 1, m), F32),
             pltpu.VMEM((n, levels + 1, m), F32),
-            pltpu.VMEM((11, levels, m), F32),
-            pltpu.VMEM((10, levels, m), F32),
-            pltpu.VMEM((10, levels, m), F32),
+            pltpu.VMEM((16, levels, m), F32),
+            pltpu.VMEM((3, levels, m), F32),
+            pltpu.VMEM((4, levels, m), F32),
+            pltpu.VMEM((4, 3, levels, m), F32),
+            pltpu.VMEM((4, 3, levels, m), F32),
+            pltpu.VMEM((2, levels, m), F32),
+            pltpu.VMEM((3, levels, m), F32),
             pltpu.VMEM((len(PHASES), 1, m), F32),
         ]
         + [pltpu.VMEM((group_size(px, py, dims) - 1, 1, m), F32) for dims in PHASES]
         + [
             pltpu.SemaphoreType.DMA((7,)),
-            pltpu.SemaphoreType.DMA((10,)),
-            pltpu.SemaphoreType.DMA((10,)),
+            pltpu.SemaphoreType.DMA((11,)),
+            pltpu.SemaphoreType.DMA((11,)),
             pltpu.SemaphoreType.DMA((len(PHASES),)),
             pltpu.SemaphoreType.DMA((len(PHASES),)),
         ],

time: 41 us -> 38.3 us (0.934)
  Pallas kernels: 40.2 us -> 37.5 us
    pallas_call x1, Pallas kernels: 38.6 us -> 36 us  [local(): pl.pallas_call(functools.partial(halo_kernel, px, py), out_shape=[pltpu.V...]
where the time goes in v4:
time: 38.3 us; the launch traced here: 38.2 us
  Pallas kernels  37.5 us (98%)
  between operations  0.64 us (2%)
    pallas_call x1, Pallas kernels, local(): pl.pallas_call(functools.partial(halo_kernel, px, py), out_shape=[pltpu.V...  36 us
    pallas_call x1, Pallas kernels, local(): pl.pallas_call(combine_kernel, out_shape=[jax.ShapeDtypeStruct(shape, F32...  1.56 us

profile of v4, /device:TPU:1, one launch (start us, length us, event | category | flops | bytes accessed | tf_op | source)
XLA Modules:
  0.0 38.2 jit_solution(7002040086980510053)
XLA Ops:
  0.6 36.0 %halo.1 = (f32[41,24,128]{2,1,0:T(8,128)S(1)}, f32[40,24,128]{2,1,0:T(8,128)S(1)}, f32[1000,128]{1,0:T(8,128)S(1)}, f32[41,24,128]{2,1,0:T(8,128)S(1)}, f32[40,2...) custom-call(bf16[3,40,24,128]{3,2,1,0:T(8,128)(2,1)} %metric_h.1, ...), custom_call_target="tpu_custom_call" | custom-call | tf_op jit(solution)/shard_map/halo/pallas_call | solution.py:498
  36.6 1.6 %combine.1 = (f32[40,24,128]{2,1,0:T(8,128)}, f32[40,24,128]{2,1,0:T(8,128)}, f32[1000,128]{1,0:T(8,128)}, f32[40,24,128]{2,1,0:T(8,128)}) custom-call(f32[41,24,128]{2,1,0:T(8,128)S(1)} %get-tuple-element.21.x_ref, f32[40,24,128]{2,1,0:T(8,128)S(1)} %get-tuple-element.22.y_ref, f32[1000,128]{1,0:T(8,128)S(1)} %get-tuple-element.23.z_ref, ...), custom_call_target="tpu_custom_call" | custom-call | tf_op jit(solution)/shard_map/combine/pallas_call | solution.py:538

commit v5 on v4

--- a/solution.py
+++ b/solution.py
@@ -10,6 +10,7 @@
 
 MESH = pl.DeviceIdType.MESH
 F32 = jnp.float32
+SPARE = 100
 
 
 def factors(px, py):
@@ -81,7 +82,7 @@
     metric_h, helm_h, forc_h, orient_h, sx_h, sy_h, sz_h,
     x_ref, y_ref, z_ref, rx, ry, rz, wx, wy, wz, p0, p1, p2, coef,
     metric, helm, forc, orient, ix_s, iy_s, iz_s, rd_s,
-    z_x, rz_x, wz_x, tb, send_b, recv_b, msg_s, msg_r, dia_s, dia_r, row_b, *rest,
+    z_x, rz_x, wz_x, tb, send_b, recv_b, msg_s, msg_r, str_s, str_r, dia_s, dia_r, row_b, *rest,
 ):
     slots = rest[: len(PHASES)]
     load_sem, send_sem, recv_sem, ar_send, ar_recv = rest[len(PHASES) :]
@@ -228,12 +229,12 @@
 
     flux = strip_flux(5, zero, zero, True)
     both = 9.0 * tb[0] * tb[1] * tb[3]
-    msg_s[2, 0] = tb[6]
-    msg_s[2, 1] = -flux[2]
-    msg_s[2, 2] = both
-    msg_s[3, 0] = -flux[3]
-    msg_s[3, 1] = 9.0 * tb[1] * tb[1] * tb[3] - 2.0 * tb[1]
-    msg_s[3, 2] = both
+    spare = lane == SPARE
+    slab = jnp.where(odd, tb[6], pltpu.roll(-flux[2], m - 1, 1))
+    str_s[0] = jnp.where(spare, pltpu.roll(both, (SPARE - 2 * n + 1) % m, 1), slab)
+    slope = 9.0 * tb[1] * tb[1] * tb[3] - 2.0 * tb[1]
+    slab = jnp.where(odd, pltpu.roll(slope, 1, 1), -flux[3])
+    str_s[1] = jnp.where(spare, pltpu.roll(both, (SPARE - 2 * n + 2) % m, 1), slab)
     msg_s[0, 0] = x_ref[0]
     msg_s[0, 1] = -row(0, start, zero, True, True)[1][0]
     msg_s[0, 2] = 9.0 * ix_s[0] * iy_s[0] * rd_s[0]
@@ -250,8 +251,10 @@
         exchange(dia_s.at[0], dia_r.at[1], 9, north_west),
         exchange(dia_s.at[1], dia_r.at[2], 10, south_east),
     ] + [
-        exchange(msg_s.at[k], msg_r.at[k], 4 + k, device)
-        for k, device in ((2, south), (3, north), (0, west), (1, east))
+        exchange(str_s.at[0], str_r.at[0], 6, south),
+        exchange(str_s.at[1], str_r.at[1], 7, north),
+        exchange(msg_s.at[0], msg_r.at[0], 4, west),
+        exchange(msg_s.at[1], msg_r.at[1], 5, east),
     ]
     pl.semaphore_wait(barrier, len(greeted))
     for copy in first:
@@ -267,18 +270,21 @@
     for copy in first:
         copy.wait_recv()
     x_ref[n] = msg_r[0, 0]
-    strip1 = pltpu.roll(msg_r[2, 0], m - 1, 1)
+    north_slab, south_slab = str_r[0], str_r[1]
+    strip1 = pltpu.roll(north_slab, m - 1, 1)
     from_east = msg_r[0, 1] + jnp.where(lane == m - 1, msg_r[0, 2] * dia_r[0], 0.0)
     from_west = (
         msg_r[1, 0]
         + msg_r[1, 1] * x_ref[0]
         + jnp.where(lane == m - 1, msg_r[1, 2] * dia_r[2], 0.0)
     )
-    from_north = msg_r[2, 1] + jnp.where(lane == 2 * n - 1, msg_r[2, 2] * dia_r[0], 0.0)
+    both = pltpu.roll(north_slab, (2 * n - 1 - SPARE) % m, 1)
+    from_north = pltpu.roll(north_slab, 1, 1) + jnp.where(lane == 2 * n - 1, both * dia_r[0], 0.0)
+    both = pltpu.roll(south_slab, (2 * n - 2 - SPARE) % m, 1)
     from_south = (
-        msg_r[3, 0]
-        + msg_r[3, 1] * pltpu.roll(tb[6], m - 1, 1)
-        + jnp.where(lane == 2 * n - 2, msg_r[3, 2] * dia_r[1], 0.0)
+        south_slab
+        + pltpu.roll(south_slab, m - 1, 1) * pltpu.roll(tb[6], m - 1, 1)
+        + jnp.where(lane == 2 * n - 2, both * dia_r[1], 0.0)
     )
     high = pltpu.roll(from_north, m - 1, 1) - strip_flux(5, x_ref[n], strip1, True)[3]
     strip2 = jnp.where(odd, pltpu.roll(from_south, 1, 1), high)
@@ -515,8 +521,10 @@
             pltpu.VMEM((16, levels, m), F32),
             pltpu.VMEM((3, levels, m), F32),
             pltpu.VMEM((4, levels, m), F32),
-            pltpu.VMEM((4, 3, levels, m), F32),
-            pltpu.VMEM((4, 3, levels, m), F32),
+            pltpu.VMEM((2, 3, levels, m), F32),
+            pltpu.VMEM((2, 3, levels, m), F32),
+            pltpu.VMEM((2, levels, m), F32),
+            pltpu.VMEM((2, levels, m), F32),
             pltpu.VMEM((2, levels, m), F32),
             pltpu.VMEM((3, levels, m), F32),
             pltpu.VMEM((len(PHASES), 1, m), F32),

time: 38.3 us -> 37.5 us (0.979)
  Pallas kernels: 37.5 us -> 36.7 us
    pallas_call x1, Pallas kernels: 36 us -> 35.2 us  [local(): pl.pallas_call(functools.partial(halo_kernel, px, py), out_shape=[pltpu.V...]
where the time goes in v5:
time: 37.5 us; the launch traced here: 37.4 us
  Pallas kernels  36.7 us (98%)
  between operations  0.64 us (2%)
    pallas_call x1, Pallas kernels, local(): pl.pallas_call(functools.partial(halo_kernel, px, py), out_shape=[pltpu.V...  35.2 us
    pallas_call x1, Pallas kernels, local(): pl.pallas_call(combine_kernel, out_shape=[jax.ShapeDtypeStruct(shape, F32...  1.56 us

profile of v5, /device:TPU:1, one launch (start us, length us, event | category | flops | bytes accessed | tf_op | source)
XLA Modules:
  0.0 37.4 jit_solution(4046465473203897311)
XLA Ops:
  0.6 35.2 %halo.1 = (f32[41,24,128]{2,1,0:T(8,128)S(1)}, f32[40,24,128]{2,1,0:T(8,128)S(1)}, f32[1000,128]{1,0:T(8,128)S(1)}, f32[41,24,128]{2,1,0:T(8,128)S(1)}, f32[40,2...) custom-call(bf16[3,40,24,128]{3,2,1,0:T(8,128)(2,1)} %metric_h.1, ...), custom_call_target="tpu_custom_call" | custom-call | tf_op jit(solution)/shard_map/halo/pallas_call | solution.py:504
  35.8 1.6 %combine.1 = (f32[40,24,128]{2,1,0:T(8,128)}, f32[40,24,128]{2,1,0:T(8,128)}, f32[1000,128]{1,0:T(8,128)}, f32[40,24,128]{2,1,0:T(8,128)}) custom-call(f32[41,24,128]{2,1,0:T(8,128)S(1)} %get-tuple-element.21.x_ref, f32[40,24,128]{2,1,0:T(8,128)S(1)} %get-tuple-element.22.y_ref, f32[1000,128]{1,0:T(8,128)S(1)} %get-tuple-element.23.z_ref, ...), custom_call_target="tpu_custom_call" | custom-call | tf_op jit(solution)/shard_map/combine/pallas_call | solution.py:546

commit v6 on v5

--- a/solution.py
+++ b/solution.py
@@ -241,10 +241,18 @@
     msg_s[1, 0] = -row(n - 1, start, zero, True, True)[1][1]
     msg_s[1, 1] = 9.0 * ix_s[n - 1] * ix_s[n - 1] * rd_s[n - 1] - 2.0 * ix_s[n - 1]
     msg_s[1, 2] = 9.0 * ix_s[n - 1] * iy_s[n - 1] * rd_s[n - 1]
-    dia_s[0] = jnp.where(
-        lane == m - 1, pltpu.roll(y_ref[0], m - 1, 1), pltpu.roll(x_ref[0], 2 * n - 1, 1)
-    )
-    dia_s[1] = pltpu.roll(y_ref[n - 1], m - 1, 1)
+    def as_row(columns):
+        spread = zero
+        for k, column in enumerate(columns):
+            spread = jnp.where(lane == level + 32 * k, column, spread)
+        return jnp.sum(spread, axis=0, keepdims=True)
+
+    def as_column(line, k):
+        return jnp.sum(jnp.where(lane == level + 32 * k, line, 0.0), axis=1, keepdims=True)
+
+    y_first, x_first, y_last = y_ref[0][:, 0:1], x_ref[0], y_ref[n - 1][:, 0:1]
+    dia_s[0] = as_row((y_first, x_first[:, 0:1], x_first[:, m - 1 :]))
+    dia_s[1] = as_row((y_last,))
     north_east, south_east, north_west, south_west = corner
     first = [
         exchange(dia_s.at[0], dia_r.at[0], 8, south_west),
@@ -270,21 +278,23 @@
     for copy in first:
         copy.wait_recv()
     x_ref[n] = msg_r[0, 0]
+    north_east_y, north_east_x = as_column(dia_r[0], 0), as_column(dia_r[0], 1)
+    south_east_x, north_west_y = as_column(dia_r[1], 2), as_column(dia_r[2], 0)
     north_slab, south_slab = str_r[0], str_r[1]
     strip1 = pltpu.roll(north_slab, m - 1, 1)
-    from_east = msg_r[0, 1] + jnp.where(lane == m - 1, msg_r[0, 2] * dia_r[0], 0.0)
+    from_east = msg_r[0, 1] + jnp.where(lane == m - 1, msg_r[0, 2] * north_east_y, 0.0)
     from_west = (
         msg_r[1, 0]
         + msg_r[1, 1] * x_ref[0]
-        + jnp.where(lane == m - 1, msg_r[1, 2] * dia_r[2], 0.0)
+        + jnp.where(lane == m - 1, msg_r[1, 2] * north_west_y, 0.0)
     )
     both = pltpu.roll(north_slab, (2 * n - 1 - SPARE) % m, 1)
-    from_north = pltpu.roll(north_slab, 1, 1) + jnp.where(lane == 2 * n - 1, both * dia_r[0], 0.0)
+    from_north = pltpu.roll(north_slab, 1, 1) + jnp.where(lane == 2 * n - 1, both * north_east_x, 0.0)
     both = pltpu.roll(south_slab, (2 * n - 2 - SPARE) % m, 1)
     from_south = (
         south_slab
         + pltpu.roll(south_slab, m - 1, 1) * pltpu.roll(tb[6], m - 1, 1)
-        + jnp.where(lane == 2 * n - 2, both * dia_r[1], 0.0)
+        + jnp.where(lane == 2 * n - 2, both * south_east_x, 0.0)
     )
     high = pltpu.roll(from_north, m - 1, 1) - strip_flux(5, x_ref[n], strip1, True)[3]
     strip2 = jnp.where(odd, pltpu.roll(from_south, 1, 1), high)
@@ -525,8 +535,8 @@
             pltpu.VMEM((2, 3, levels, m), F32),
             pltpu.VMEM((2, levels, m), F32),
             pltpu.VMEM((2, levels, m), F32),
-            pltpu.VMEM((2, levels, m), F32),
-            pltpu.VMEM((3, levels, m), F32),
+            pltpu.VMEM((2, 1, m), F32),
+            pltpu.VMEM((3, 1, m), F32),
             pltpu.VMEM((len(PHASES), 1, m), F32),
         ]
         + [pltpu.VMEM((group_size(px, py, dims) - 1, 1, m), F32) for dims in PHASES]

time: 37.5 us -> 37.2 us (level)
  no operation moved by 1% of the time
where the time goes in v6:
time: 37.2 us; the launch traced here: 37 us
  Pallas kernels  36.4 us (98%)
  between operations  0.64 us (2%)
    pallas_call x1, Pallas kernels, local(): pl.pallas_call(functools.partial(halo_kernel, px, py), out_shape=[pltpu.V...  34.8 us
    pallas_call x1, Pallas kernels, local(): pl.pallas_call(combine_kernel, out_shape=[jax.ShapeDtypeStruct(shape, F32...  1.56 us

profile of v6, /device:TPU:1, one launch (start us, length us, event | category | flops | bytes accessed | tf_op | source)
XLA Modules:
  0.0 37.0 jit_solution(14511882095864143226)
XLA Ops:
  0.6 34.8 %halo.1 = (f32[41,24,128]{2,1,0:T(8,128)S(1)}, f32[40,24,128]{2,1,0:T(8,128)S(1)}, f32[1000,128]{1,0:T(8,128)S(1)}, f32[41,24,128]{2,1,0:T(8,128)S(1)}, f32[40,2...) custom-call(bf16[3,40,24,128]{3,2,1,0:T(8,128)(2,1)} %metric_h.1, ...), custom_call_target="tpu_custom_call" | custom-call | tf_op jit(solution)/shard_map/halo/pallas_call | solution.py:514
  35.5 1.6 %combine.1 = (f32[40,24,128]{2,1,0:T(8,128)}, f32[40,24,128]{2,1,0:T(8,128)}, f32[1000,128]{1,0:T(8,128)}, f32[40,24,128]{2,1,0:T(8,128)}) custom-call(f32[41,24,128]{2,1,0:T(8,128)S(1)} %get-tuple-element.21.x_ref, f32[40,24,128]{2,1,0:T(8,128)S(1)} %get-tuple-element.22.y_ref, f32[1000,128]{1,0:T(8,128)S(1)} %get-tuple-element.23.z_ref, ...), custom_call_target="tpu_custom_call" | custom-call | tf_op jit(solution)/shard_map/combine/pallas_call | solution.py:556
